TPU v7x, 256 devices: a whole 4x4x8 slice. The times are simulated.
256 devices in a mesh: seq: 64 (over x, y, z_lo), head: 4 (over z_hi, core).
Axes of the slice: x: 4, y: 4, z: 8 (z_hi: 2, z_lo: 4; z = z_hi * 4 + z_lo), core: 2. Of those that a mesh axis runs over, the one named last changes fastest.
Arguments:
- prompt_token_query: bfloat16 [2048, 8192], P('seq', 'head'), may hold values from -6 to 6
- prompt_token_key: bfloat16 [2048, 1024], P('seq', 'head'), may hold values from -6 to 6
- prompt_token_value: bfloat16 [2048, 1024], P('seq', 'head'), may hold values from -6 to 6
- response_query_slots: bfloat16 [12288, 8192], P('seq', 'head'), may hold values from -160 to 160
- response_key_slots: bfloat16 [12288, 1024], P('seq', 'head'), may hold values from -6 to 6
- response_value_slots: bfloat16 [12288, 1024], P('seq', 'head'), may hold values from -6 to 6
- lengths: int32 [16], replicated, may hold values from 1 to 32, 64 in all
- block_table: int32 [64], replicated, may hold values from 0 to 63, each once
Outputs:
- prompt_out: bfloat16 [2048, 8192], P(('seq', 'head'))
- answer_out: bfloat16 [12288, 8192], P(('seq', 'head'))
Inputs may be any that keep to these rules, and one draw needn't show every extreme that they name: `lengths`: they sum to 64; the largest is exactly 32. `block_table`: A permutation of 0 to 63.
All inputs are finite; a program needn't handle non-finite values.
Results may differ from a plain program's by a relative error of at most 0.007.
Values may be sent and summed in bfloat16 or wider, within the bound.
No kernel may reach another device: no remote copies, remote signals or barrier semaphores. Data moves between devices by JAX's collectives and lax.ppermute only.
A program may use at most 64 MiB of HBM per device.

v0:
```python
import functools

import jax
import jax.numpy as jnp
from jax import lax
from jax.experimental import pallas as pl
from jax.experimental.pallas import tpu as pltpu
from jax.sharding import Mesh, PartitionSpec as P


D = 128
RB = 192
PR = 32
G = 8
CH = 512
LIMIT = 36 * 2**20
PER_EXP = 128 ** -0.5 * 1.4426950408889634
NEG = -1e30
RING = (((0, 0, 4),), ((3, 0, 4), (1, 0, 4)), ((2, 0, 2), (2, 2, 2)))


def homes_of(groups):
    return [(colour, *h) for g in groups for colour in range(2) for h in RING[g]]


def kernel(place_ref, tab_ref, own_ref, got_ref, *refs, groups, last, region, mh):
    first = 0 in groups
    homes = homes_of(groups)
    pieces, refs = refs[:len(homes)], refs[len(homes):]
    if not first:
        before, refs = refs[:4], refs[4:]
    if last:
        out_ref, refs = refs[0], refs[1:]
    m, a, pm, pa, kv, flags, qs, pqs, s0, s1, p0, p1, f0, f1 = refs
    px, py, pp, side = [place_ref[i] for i in range(4)]
    pair = (px * 4 + py) * 2 + pp
    prompts = sum(2 * n * PR for _, _, _, n in homes)
    per = G // mh

    spans = [(place_ref[4 + t], place_ref[6 + t]) for t in range(2)]
    flags[:CH] = jnp.ones((CH, D), jnp.bfloat16)
    flags[CH:] = jnp.zeros((CH, D), jnp.bfloat16)

    def block(piece, r, t, i):
        kv[pl.ds(pl.multiple_of(t * region + prompts + i * RB, 64), RB), :] = piece[r, PR:, :]

    counts = (jnp.int32(0), jnp.int32(0))
    at = 0
    for piece, (colour, far, lead, n) in zip(pieces, homes):
        def bring(i, counts, piece=piece, colour=colour, far=far, lead=lead, at=at):
            near, e = i >> 1, i & 1
            dx, dy = (lead + near, far) if colour == 0 else (far, lead + near)
            slot = ((((px + dx) & 3) * 4 + ((py + dy) & 3)) * 2 + (pp ^ colour)) * 2 + (side ^ e)
            g = tab_ref[slot]
            new = []
            for t in range(2):
                kv[pl.ds(pl.multiple_of(t * region + (at + i) * PR, PR), PR), :] = piece[i, :PR, :]
                own, start = spans[t]
                hit = (g >= start) & (g < own)

                @pl.when(hit)
                def fetch(t=t):
                    block(piece, i, t, counts[t])

                new.append(counts[t] + hit.astype(jnp.int32))
            return tuple(new)

        counts = lax.fori_loop(0, 2 * n, bring, counts)
        at += 2 * n
    if first:
        for t in range(2):
            block(pieces[0], side ^ t, t, counts[t])
        counts = tuple(c + 1 for c in counts)
    keys = [prompts + c * RB for c in counts]
    chunks = [(k + CH - 1) // CH for k in keys]

    for src, t in ((own_ref, side), (got_ref, 1 - side)):
        for h in range(G):
            cols = slice(h * D, (h + 1) * D)
            qs[t * per + h // mh, pl.ds(h % mh * RB, RB)] = src[PR:, cols]
            pqs[pl.ds((t * G + h) * PR, PR)] = src[:PR, cols]
    if first:
        for r in (m, pm):
            r[...] = jnp.full(r.shape, NEG, jnp.float32)
        for r in (a, pa):
            r[...] = jnp.zeros(r.shape, jnp.float32)
    else:
        for r, b in zip((m, a, pm, pa), before):
            r[...] = b[...]
    for t in range(2):
        def pad(i, c, t=t):
            rows = pl.ds(pl.multiple_of(t * region + i * 64, 64), 64)
            kv[rows, :D] = kv[pl.ds(t * region, 64), :D]
            kv[rows, D:] = jnp.zeros((64, D), jnp.bfloat16)
            return c

        lax.fori_loop(keys[t] // 64, chunks[t] * (CH // 64), pad, 0)

    def soft(s, m_ref, i):
        old = m_ref[i]
        new = jnp.maximum(old, jnp.max(s, axis=1, keepdims=True))
        m_ref[i] = new
        spread = jnp.concatenate([new] * (s.shape[1] // D), axis=1)
        return jnp.exp2((s - spread) * PER_EXP).astype(jnp.bfloat16), jnp.exp2((old - new) * PER_EXP)

    def scores(q, start, n):
        return lax.dot_general(q, kv[pl.ds(start, n), :D], (((1,), (1,)), ((), ())), preferred_element_type=jnp.float32)

    def mixed(p, start, n, flag):
        v = jnp.concatenate([kv[pl.ds(start, n), D:], flag], axis=1)
        return lax.dot_general(p, v, (((1,), (0,)), ((), ())), preferred_element_type=jnp.float32)

    def both(f):
        return jnp.concatenate([f, f], axis=1)

    where = []
    for colour, far, lead, n in homes:
        lane = lax.broadcasted_iota(jnp.int32, (1, 2 * n * PR), 1)
        near, e = lead + (lane >> 6), (lane >> 5) & 1
        dx, dy = (near, jnp.int32(far)) if colour == 0 else (jnp.int32(far), near)
        slot = ((((px + dx) & 3) * 4 + ((py + dy) & 3)) * 2 + (pp ^ colour)) * 2 + (side ^ e)
        where.append(slot * PR + (lane & (PR - 1)))
    where = jnp.concatenate(where, axis=1)
    half = G * PR
    for t in range(2):
        row = (lax.broadcasted_iota(jnp.int32, (half, 1), 0) & (PR - 1)) + (2 * pair + t) * PR
        s = jnp.where(where <= row, scores(pqs[t * half:(t + 1) * half], 0, prompts), NEG)
        p, factor = soft(s, pm, t)
        pa[t] = pa[t] * both(factor) + mixed(p, 0, prompts, jnp.ones((prompts, D), jnp.bfloat16))

    split, total = chunks[0] * per, (chunks[0] + chunks[1]) * per
    shift = per.bit_length() - 1

    def unit(u):
        t = (u >= split).astype(jnp.int32)
        v = u - t * split
        c, h = v >> shift, v & (per - 1)
        return t, c, t * per + h, pl.multiple_of(t * region + c * CH, CH)

    def stage_a(u, s):
        _, _, i, start = unit(u)
        s[...] = scores(qs[i], start, CH)

    def stage_b(u, s, p, f):
        t, c, i, _ = unit(u)
        x = s[...]
        if first:
            key = lax.broadcasted_iota(jnp.int32, (mh * RB, CH), 1)
            row = lax.broadcasted_iota(jnp.int32, (mh * RB, 1), 0)
            row = row % RB + (jnp.where(t == 0, keys[0], keys[1]) - RB - c * CH)
            x = jnp.where(key <= row, x, NEG)
        p[...], f[...] = soft(x, m, i)

    def stage_c(u, p, f):
        t, c, i, start = unit(u)
        live = jnp.minimum(jnp.where(t == 0, keys[0], keys[1]) - c * CH, CH)
        flag = flags[pl.ds(pl.multiple_of(CH - live, 64), CH), :]
        a[i] = a[i] * both(f[...]) + mixed(p[...], start, CH, flag)

    stage_a(0, s0)
    p1[...] = jnp.zeros(p1.shape, p1.dtype)
    f1[...] = jnp.ones(f1.shape, f1.dtype)

    def two(i, c):
        u = 2 * i
        stage_a(u + 1, s1)
        stage_b(u, s0, p0, f0)
        stage_c(jnp.maximum(u - 1, 0), p1, f1)
        stage_a(jnp.minimum(u + 2, total - 1), s0)
        stage_b(u + 1, s1, p1, f1)
        stage_c(u, p0, f0)
        return c

    lax.fori_loop(0, total >> 1, two, 0)
    stage_c(total - 1, p1, f1)

    if last:
        parts = out_ref.shape[0] // 2
        pn, rn = PR // parts, RB // parts
        for t in range(2):
            for h in range(G):
                cols = slice(h * D, (h + 1) * D)
                i, top = t * per + h // mh, h % mh * RB
                done = (a[i, top:top + RB, :D] / a[i, top:top + RB, D:]).astype(jnp.bfloat16)
                rr = slice(h * PR, (h + 1) * PR)
                asked = (pa[t, rr, :D] / pa[t, rr, D:]).astype(jnp.bfloat16)
                for d in range(parts):
                    out_ref[2 * d + t, :pn, cols] = asked[d * pn:(d + 1) * pn]
                    out_ref[2 * d + t, pn:, cols] = done[d * rn:(d + 1) * rn]


def attention(place, table, own, got, pieces, state, groups, parts, mh):
    slots = table.shape[0]
    f32, bf16 = jnp.float32, jnp.bfloat16
    smem = pl.BlockSpec(memory_space=pltpu.SMEM)
    vmem = pl.BlockSpec(memory_space=pltpu.VMEM)
    last = 2 in groups
    count = sum(2 * n for *_, n in homes_of(groups))
    region = -(-(count * PR + min(count, slots // 2) * RB) // CH) * CH
    units = 2 * G // mh
    shapes = [(units, mh * RB, D), (units, mh * RB, 2 * D), (2, G * PR, D), (2, G * PR, 2 * D)]
    state = [x.reshape(shape) for x, shape in zip(state, shapes)]
    inputs = [place, table, own, got, *pieces, *state]
    kept = [jax.ShapeDtypeStruct(s, f32) for s in shapes]
    if last:
        out_shape, out_specs = jax.ShapeDtypeStruct((2 * parts, (PR + RB) // parts, G * D), bf16), vmem
    else:
        out_shape, out_specs = kept, [vmem] * 4
    flops = 4 * RB * G * 2 * D * (count * (PR + RB // 2))
    return pl.pallas_call(
        functools.partial(kernel, groups=groups, last=last, region=region, mh=mh),
        out_shape=out_shape,
        in_specs=[smem, smem] + [vmem] * (len(inputs) - 2),
        out_specs=out_specs,
        scratch_shapes=([pltpu.VMEM(s, f32) for s in shapes] if last else []) + [
            pltpu.VMEM((2 * region, 2 * D), bf16),
            pltpu.VMEM((2 * CH, D), bf16),
            pltpu.VMEM((units, mh * RB, D), bf16),
            pltpu.VMEM((2 * G * PR, D), bf16),
            pltpu.VMEM((mh * RB, CH), f32), pltpu.VMEM((mh * RB, CH), f32),
            pltpu.VMEM((mh * RB, CH), bf16), pltpu.VMEM((mh * RB, CH), bf16),
            pltpu.VMEM((mh * RB, D), f32), pltpu.VMEM((mh * RB, D), f32),
        ],
        cost_estimate=pl.CostEstimate(flops=flops, transcendentals=flops // 512, bytes_accessed=2**23),
        compiler_params=pltpu.CompilerParams(vmem_limit_bytes=LIMIT),
        name="attention",
    )(*inputs)


def attend(place, table, own, got, gathered, parts):
    gathered = [[p.reshape(-1, *p.shape[2:]) for p in c] for c in gathered]
    run = functools.partial(attention, place, table, own, got)
    state = run([c[0] for c in gathered], (), (0,), parts, 2)
    state = run([p for c in gathered for p in c[1:3]], state, (1,), parts, 4)
    return run([p for c in gathered for p in c[3:]], state, (2,), parts, 4)


def together(copies):
    for c in copies:
        c.start()
    for c in copies:
        c.wait()


def sort_keys(side_ref, pk, pv, rk, rv, here, there, sems):
    side = side_ref[0]
    copies = []
    for out, j in ((here, side), (there, 1 - side)):
        for rows, k, v in ((pl.ds(0, PR), pk, pv), (pl.ds(PR, RB), rk, rv)):
            for w, src in enumerate((k, v)):
                copies.append(pltpu.make_async_copy(
                    src.at[:, pl.ds(pl.multiple_of(j * D, D), D)], out.at[rows, pl.ds(w * D, D)], sems.at[len(copies)]))
    together(copies)


def sort_queries(side_ref, pq, rq, keep, give, sems):
    side, half = side_ref[0], keep.shape[1]
    copies = []
    for out, j in ((keep, side), (give, 1 - side)):
        for rows, src in ((pl.ds(0, PR), pq), (pl.ds(PR, RB), rq)):
            copies.append(pltpu.make_async_copy(
                src.at[:, pl.ds(pl.multiple_of(j * half, half), half)], out.at[rows], sems.at[len(copies)]))
    together(copies)


def sorted_by_side(body, side, arrays, cols):
    out = jax.ShapeDtypeStruct((PR + RB, cols), jnp.bfloat16)
    vmem = pl.BlockSpec(memory_space=pltpu.VMEM)
    return pl.pallas_call(
        body, out_shape=(out, out),
        in_specs=[pl.BlockSpec(memory_space=pltpu.SMEM)] + [pl.BlockSpec(memory_space=pltpu.HBM)] * len(arrays),
        out_specs=(vmem, vmem), scratch_shapes=[pltpu.SemaphoreType.DMA((2 * len(arrays),))],
        compiler_params=pltpu.CompilerParams(vmem_limit_bytes=8 * 2**20),
    )(side.reshape(1), *arrays)


SEQ = ("x", "y", "zp", "zq")
HEAD = ("zh", "core")


def whole(pq, pk, pv, rq, rk, rv, lengths, table):
    side = lax.axis_index("zq").astype(jnp.int32)
    place = [lax.axis_index(n).astype(jnp.int32) for n in SEQ]
    mates = lax.dynamic_slice_in_dim(table, (place[0] * 4 + place[1]) * 4 + place[2] * 2, 2, 0)
    ends = jnp.cumsum(lengths)
    begun = jnp.where(mates[:, None] >= ends[None, :], ends[None, :], 0)
    place = jnp.concatenate([jnp.stack(place), mates, jnp.max(begun, axis=1)])
    here, there = sorted_by_side(sort_keys, side, (pk, pv, rk, rv), 2 * D)
    keep, give = sorted_by_side(sort_queries, side, (pq, rq), rq.shape[1] // 2)
    swap = [(0, 1), (1, 0)]
    next_to = lax.ppermute(there, "zq", swap)
    far_same = lax.ppermute(here, "zp", swap)
    far_other = lax.ppermute(there, ("zp", "zq"), [(i, 3 - i) for i in range(4)])

    far_other, give = lax.optimization_barrier((far_other, give))
    got = lax.ppermute(give, "zq", swap)

    def ring(t, axis):
        up, down = [(i, (i + 1) % 4) for i in range(4)], [(i, (i - 1) % 4) for i in range(4)]
        before, after = lax.ppermute(t, axis, up), lax.ppermute(t, axis, down)
        n = t.shape[0] // 2
        return t, before, after, lax.ppermute(before[:n], axis, up), lax.ppermute(after[n:], axis, down)

    def colour(t, first, second):
        own, before, after, half_a, half_b = ring(t, first)
        return ring(jnp.stack([own, after, jnp.concatenate([half_a, half_b], axis=0), before]), second)

    gathered = (colour(jnp.stack([here, next_to]), "x", "y"), colour(jnp.stack([far_same, far_other]), "y", "x"))
    parts = lax.axis_size(HEAD)
    mixed = attend(place, table, keep, got, gathered, parts)
    back = lax.all_to_all(mixed, HEAD + ("zq",), split_axis=0, concat_axis=0, tiled=True)
    pn = PR // parts
    flat = lambda t: t.transpose(1, 0, 2).reshape(t.shape[1], -1)
    return flat(back[:, :pn]), flat(back[:, pn:])


def solution(mesh):
    grid = Mesh(mesh.devices.reshape(4, 4, 2, 2, 2, 2), SEQ + HEAD)
    both = P(SEQ, HEAD)
    rows = P(SEQ + HEAD, None)
    return jax.shard_map(whole, mesh=grid, in_specs=(both,) * 6 + (P(), P()), out_specs=(rows, rows), check_vma=False)
```

profile of v0, /device:TPU:57, one launch (start us, length us, event | category | flops | bytes accessed | tf_op | source)
XLA Modules:
  0.0 137.3 jit_solution(6002733876739922759)
XLA Ops:
  0.6 0.9 copy-done.2
  1.5 0.9 copy-done.3
  4.0 1.7 %collective-permute-start = (bf16[224,256]{1,0:T(8,128)(2,1)S(1)}, bf16[224,256]{1,0:T(8,128)(2,1)S(1)}, u32[]{:S(2)}, u32[]{:S(2)}) collective-permute-start(bf16[224,256]{1,0:T(8,128)(2,1)S(1)} %get-tuple-element.17), channel_id=1, source_target_pairs={{0,12},{4,8},{8,4},{12,0},{1,13},{5,9},{9,5},{13,1},{2,14},{6,10},... | collective-permute-start | bytes 344072 | tf_op jit(solution)/shard_map/ppermute | solution.py:293
  5.7 1.5 %collective-permute-start.11 = (bf16[224,256]{1,0:T(8,128)(2,1)S(1)}, bf16[224,256]{1,0:T(8,128)(2,1)S(1)}, u32[]{:S(2)}, u32[]{:S(2)}) collective-permute-start(bf16[224,256]{1,0:T(8,128)(2,1)S(1)} %get-tuple-element.20), channel_id=1, source_target_pairs={{0,8},{8,0},{1,9},{9,1},{2,10},{10,2},{3,11},{11,3},{4,12},{12,4},... | collective-permute-start | bytes 344072 | tf_op jit(solution)/shard_map/ppermute | solution.py:292
  7.2 1.1 collective-permute-start.2
  8.3 1.1 copy-done
  9.4 0.9 copy-done.1
  10.3 0.9 shard_map.95
  11.2 1.4 %collective-permute-done = bf16[224,256]{1,0:T(8,128)(2,1)S(1)} collective-permute-done((bf16[224,256]{1,0:T(8,128)(2,1)S(1)}, bf16[224,256]{1,0:T(8,128)(2,1)S(1)}, u32[]{:S(2)}, u32[]{:S(2)}) %collective-permute-start) | collective-permute-done | bytes 114720 | tf_op jit(solution)/shard_map/ppermute | solution.py:293
  12.6 2.3 %collective-permute-done.11 = bf16[224,256]{1,0:T(8,128)(2,1)S(1)} collective-permute-done((bf16[224,256]{1,0:T(8,128)(2,1)S(1)}, bf16[224,256]{1,0:T(8,128)(2,1)S(1)}, u32[]{:S(2)}, u32[]{:S(2)}) %collective-permute-start.11) | collective-permute-done | bytes 114720 | tf_op jit(solution)/shard_map/ppermute | solution.py:292
  15.1 1.5 %collective-permute-start.12 = (bf16[2,224,256]{2,1,0:T(8,128)(2,1)S(1)}, bf16[2,224,256]{2,1,0:T(8,128)(2,1)S(1)}, u32[]{:S(2)}, u32[]{:S(2)}) collective-permute-start(bf16[2,224,256]{2,1,0:T(8,128)(2,1)S(1)} %get-tuple-element.31), channel_id=1, source_target_pairs={{0,48},{16,0},{32,16},{48,32},{1,49},{17,1},{33,17},{49,33},{2,50}... | collective-permute-start | bytes 688136 | tf_op jit(solution)/shard_map/ppermute | solution.py:300
  16.6 1.3 collective-permute-start.4
  17.8 1.5 %collective-permute-start.3 = (bf16[2,224,256]{2,1,0:T(8,128)(2,1)S(1)}, bf16[2,224,256]{2,1,0:T(8,128)(2,1)S(1)}, u32[]{:S(2)}, u32[]{:S(2)}) collective-permute-start(bf16[2,224,256]{2,1,0:T(8,128)(2,1)S(1)} %get-tuple-element.33), channel_id=1, source_target_pairs={{0,192},{64,0},{128,64},{192,128},{1,193},{65,1},{129,65},{193,129... | collective-permute-start | bytes 688136 | tf_op jit(solution)/shard_map/ppermute | solution.py:300
  19.3 1.4 collective-permute-done.13
  20.7 1.4 collective-permute-start.14
  23.6 2.2 %collective-permute-start.6 = (bf16[1,224,256]{2,1,0:T(8,128)(2,1)S(1)}, bf16[1,224,256]{2,1,0:T(8,128)(2,1)S(1)}, u32[]{:S(2)}, u32[]{:S(2)}) collective-permute-start(bf16[1,224,256]{2,1,0:T(8,128)(2,1)S(1)} %slice.41), channel_id=1, source_target_pairs={{0,192},{64,0},{128,64},{192,128},{1,193},{65,1},{129,65},{193,129... | collective-permute-start | bytes 344072 | tf_op jit(solution)/shard_map/ppermute | solution.py:302
  25.9 1.1 collective-permute-done.15
  27.1 1.3 collective-permute-start.16
  28.4 1.5 %collective-permute-start.18 = (bf16[4,2,224,256]{3,2,1,0:T(8,128)(2,1)S(1)}, bf16[4,2,224,256]{3,2,1,0:T(8,128)(2,1)}, u32[]{:S(2)}, u32[]{:S(2)}) collective-permute-start(bf16[4,2,224,256]{3,2,1,0:T(8,128)(2,1)S(1)} %pad_maximum_fusion.1), channel_id=1, source_target_pairs={{0,192},{64,0},{128,64},{192,128},{1,193},{65,1},{129,65},{193,129... | collective-permute-start | bytes 2752520 | tf_op jit(solution)/shard_map/ppermute | solution.py:300
  30.0 0.8 collective-permute-start.7
  31.6 2.3 %collective-permute-start.1 = (bf16[224,1024]{1,0:T(8,128)(2,1)}, bf16[224,1024]{1,0:T(8,128)(2,1)}, u32[]{:S(2)}, u32[]{:S(2)}) collective-permute-start(bf16[224,1024]{1,0:T(8,128)(2,1)} %get-tuple-element.19), channel_id=1, source_target_pairs={{0,4},{4,0},{1,5},{5,1},{2,6},{6,2},{3,7},{7,3},{8,12},{12,8},{9,1... | collective-permute-start | bytes 1376264 | tf_op jit(solution)/shard_map/ppermute | solution.py:296
  34.5 5.9 %collective-permute-done.1.got_ref = bf16[224,1024]{1,0:T(8,128)(2,1)} collective-permute-done((bf16[224,1024]{1,0:T(8,128)(2,1)}, bf16[224,1024]{1,0:T(8,128)(2,1)}, u32[]{:S(2)}, u32[]{:S(2)}) %collective-permute-start.1) | collective-permute-done | bytes 458784 | tf_op jit(solution)/shard_map/ppermute | solution.py:296
  40.4 18.2 %attention.3 = (f32[8,384,128]{2,1,0:T(8,128)S(1)}, f32[8,384,256]{2,1,0:T(8,128)S(1)}, f32[2,256,128]{2,1,0:T(8,128)S(1)}, f32[2,256,256]{2,1,0:T(8,128)S(1)}) custom-call(s32[8]{0:T(128)S(1)} %concatenate.9.place_ref, s32[64]{0:T(128)S(1)} %copy-done.6, bf16[224,1024]{1,0:T(8,128)(2,1)S(1)} %get-tuple-element.16.own_ref, ...), custom_call_target="tpu_custom_call" | custom-call | flops 3221225472 | bytes 8388608 | tf_op jit(solution)/shard_map/attention/pallas_call | solution.py:210
  58.8 1.1 slice.47
  59.8 2.7 %collective-permute-start.19 = (bf16[2,2,224,256]{3,2,1,0:T(8,128)(2,1)S(1)}, bf16[2,2,224,256]{3,2,1,0:T(8,128)(2,1)S(1)}, u32[]{:S(2)}, u32[]{:S(2)}) collective-permute-start(bf16[2,2,224,256]{3,2,1,0:T(8,128)(2,1)S(1)} %slice.47), channel_id=1, source_target_pairs={{0,192},{64,0},{128,64},{192,128},{1,193},{65,1},{129,65},{193,129... | collective-permute-start | bytes 1376264 | tf_op jit(solution)/shard_map/ppermute | solution.py:302
  62.6 1.0 slice.42
  63.7 1.1 slice.43
  64.8 1.5 %collective-permute-start.10 = (bf16[2,2,224,256]{3,2,1,0:T(8,128)(2,1)S(1)}, bf16[2,2,224,256]{3,2,1,0:T(8,128)(2,1)S(1)}, u32[]{:S(2)}, u32[]{:S(2)}) collective-permute-start(bf16[2,2,224,256]{3,2,1,0:T(8,128)(2,1)S(1)} %slice.43), channel_id=1, source_target_pairs={{0,48},{16,0},{32,16},{48,32},{1,49},{17,1},{33,17},{49,33},{2,50}... | collective-permute-start | bytes 1376264 | tf_op jit(solution)/shard_map/ppermute | solution.py:302
  66.3 19.0 %attention.4 = (f32[4,768,128]{2,1,0:T(8,128)S(1)}, f32[4,768,256]{2,1,0:T(8,128)S(1)}, f32[2,256,128]{2,1,0:T(8,128)S(1)}, f32[2,256,256]{2,1,0:T(8,128)S(1)}) custom-call(s32[8]{0:T(128)S(1)} %concatenate.9.place_ref, s32[64]{0:T(128)S(1)} %copy-done.6, bf16[224,1024]{1,0:T(8,128)(2,1)S(1)} %get-tuple-element.16.own_ref, ...), custom_call_target="tpu_custom_call" | custom-call | flops 6442450944 | bytes 8388608 | tf_op jit(solution)/shard_map/attention/pallas_call | solution.py:210
  85.4 12.4 %attention.5 = bf16[8,56,1024]{2,1,0:T(8,128)(2,1)S(1)} custom-call(s32[8]{0:T(128)S(1)} %concatenate.9.place_ref, s32[64]{0:T(128)S(1)} %copy-done.6, bf16[224,1024]{1,0:T(8,128)(2,1)S(1)} %get-tuple-element.16.own_ref, bf16[224,1024]{1,0:T(8,128)(2,1)} %collective-permute-done.1.got_ref, bf16[4,224,256]{2,1,0:T(8,128)(2,1)S(1)} %bitcast.46, ...), custom_call_target="tpu_custom_call" | custom-call | flops 3221225472 | bytes 8388608 | tf_op jit(solution)/shard_map/attention/pallas_call | solution.py:210
  97.8 37.9 %all_to_all.5 = bf16[8,56,1024]{2,1,0:T(8,128)(2,1)S(1)} all-to-all(bf16[8,56,1024]{2,1,0:T(8,128)(2,1)S(1)} %attention.5), channel_id=1, replica_groups=mesh['x'=4,'y'=4,'zp'=2,'zq'=2,'zh'=2,'core'=2] {'zh','core','zq'}, dimensions={0} | all-to-all | bytes 1835008 | tf_op jit(solution)/shard_map/all_to_all | solution.py:311
  135.7 0.9 copy.15
  (53 shorter events, 5.9 us)
Async XLA Ops:
  0.6 0.9 copy-start.2
  1.5 0.9 copy-start.3
  2.4 0.7 copy-start.4
  3.1 0.7 copy-start.5
  4.0 8.6 %collective-permute-start = (bf16[224,256]{1,0:T(8,128)(2,1)S(1)}, bf16[224,256]{1,0:T(8,128)(2,1)S(1)}, u32[]{:S(2)}, u32[]{:S(2)}) collective-permute-start(bf16[224,256]{1,0:T(8,128)(2,1)S(1)} %get-tuple-element.17), channel_id=1, source_target_pairs={{0,12},{4,8},{8,4},{12,0},{1,13},{5,9},{9,5},{13,1},{2,14},{6,10},... | collective-permute-start | bytes 344072 | tf_op jit(solution)/shard_map/ppermute | solution.py:293
  5.7 9.2 %collective-permute-start.11 = (bf16[224,256]{1,0:T(8,128)(2,1)S(1)}, bf16[224,256]{1,0:T(8,128)(2,1)S(1)}, u32[]{:S(2)}, u32[]{:S(2)}) collective-permute-start(bf16[224,256]{1,0:T(8,128)(2,1)S(1)} %get-tuple-element.20), channel_id=1, source_target_pairs={{0,8},{8,0},{1,9},{9,1},{2,10},{10,2},{3,11},{11,3},{4,12},{12,4},... | collective-permute-start | bytes 344072 | tf_op jit(solution)/shard_map/ppermute | solution.py:292
  7.2 9.3 %collective-permute-start.2 = (bf16[224,256]{1,0:T(8,128)(2,1)S(1)}, bf16[224,256]{1,0:T(8,128)(2,1)S(1)}, u32[]{:S(2)}, u32[]{:S(2)}) collective-permute-start(bf16[224,256]{1,0:T(8,128)(2,1)S(1)} %get-tuple-element.17), channel_id=1, source_target_pairs={{0,4},{4,0},{1,5},{5,1},{2,6},{6,2},{3,7},{7,3},{8,12},{12,8},{9,1... | collective-permute-start | bytes 344072 | tf_op jit(solution)/shard_map/ppermute | solution.py:291
  8.3 1.1 copy-start
  9.4 0.9 copy-start.1
  14.9 19.0 %copy-start.7 = (s32[16]{0:T(128)S(1)}, s32[16]{0:T(128)}, u32[]{:S(2)}) copy-start(s32[16]{0:T(128)} %param.14) | copy-start | bytes 196
  15.0 19.2 %copy-start.6 = (s32[64]{0:T(128)S(1)}, s32[64]{0:T(128)}, u32[]{:S(2)}) copy-start(s32[64]{0:T(128)} %tab_ref.5) | copy-start | bytes 772
  15.0 5.7 %collective-permute-start.13 = (bf16[2,224,256]{2,1,0:T(8,128)(2,1)S(1)}, bf16[2,224,256]{2,1,0:T(8,128)(2,1)S(1)}, u32[]{:S(2)}, u32[]{:S(2)}) collective-permute-start(bf16[2,224,256]{2,1,0:T(8,128)(2,1)S(1)} %get-tuple-element.31), channel_id=1, source_target_pairs={{0,16},{16,32},{32,48},{48,0},{1,17},{17,33},{33,49},{49,1},{2,18}... | collective-permute-start | bytes 688136 | tf_op jit(solution)/shard_map/ppermute | solution.py:300
  15.1 7.0 %collective-permute-start.12 = (bf16[2,224,256]{2,1,0:T(8,128)(2,1)S(1)}, bf16[2,224,256]{2,1,0:T(8,128)(2,1)S(1)}, u32[]{:S(2)}, u32[]{:S(2)}) collective-permute-start(bf16[2,224,256]{2,1,0:T(8,128)(2,1)S(1)} %get-tuple-element.31), channel_id=1, source_target_pairs={{0,48},{16,0},{32,16},{48,32},{1,49},{17,1},{33,17},{49,33},{2,50}... | collective-permute-start | bytes 688136 | tf_op jit(solution)/shard_map/ppermute | solution.py:300
  16.6 6.5 %collective-permute-start.4 = (bf16[2,224,256]{2,1,0:T(8,128)(2,1)S(1)}, bf16[2,224,256]{2,1,0:T(8,128)(2,1)S(1)}, u32[]{:S(2)}, u32[]{:S(2)}) collective-permute-start(bf16[2,224,256]{2,1,0:T(8,128)(2,1)S(1)} %get-tuple-element.33), channel_id=1, source_target_pairs={{0,64},{64,128},{128,192},{192,0},{1,65},{65,129},{129,193},{193,1... | collective-permute-start | bytes 688136 | tf_op jit(solution)/shard_map/ppermute | solution.py:300
  17.8 5.8 %collective-permute-start.3 = (bf16[2,224,256]{2,1,0:T(8,128)(2,1)S(1)}, bf16[2,224,256]{2,1,0:T(8,128)(2,1)S(1)}, u32[]{:S(2)}, u32[]{:S(2)}) collective-permute-start(bf16[2,224,256]{2,1,0:T(8,128)(2,1)S(1)} %get-tuple-element.33), channel_id=1, source_target_pairs={{0,192},{64,0},{128,64},{192,128},{1,193},{65,1},{129,65},{193,129... | collective-permute-start | bytes 688136 | tf_op jit(solution)/shard_map/ppermute | solution.py:300
  20.7 5.2 %collective-permute-start.14 = (bf16[1,224,256]{2,1,0:T(8,128)(2,1)S(1)}, bf16[1,224,256]{2,1,0:T(8,128)(2,1)S(1)}, u32[]{:S(2)}, u32[]{:S(2)}) collective-permute-start(bf16[1,224,256]{2,1,0:T(8,128)(2,1)S(1)} %slice.44), channel_id=1, source_target_pairs={{0,16},{16,32},{32,48},{48,0},{1,17},{17,33},{33,49},{49,1},{2,18}... | collective-permute-start | bytes 344072 | tf_op jit(solution)/shard_map/ppermute | solution.py:302
  22.0 4.9 %collective-permute-start.15 = (bf16[1,224,256]{2,1,0:T(8,128)(2,1)S(1)}, bf16[1,224,256]{2,1,0:T(8,128)(2,1)S(1)}, u32[]{:S(2)}, u32[]{:S(2)}) collective-permute-start(bf16[1,224,256]{2,1,0:T(8,128)(2,1)S(1)} %slice.45), channel_id=1, source_target_pairs={{0,48},{16,0},{32,16},{48,32},{1,49},{17,1},{33,17},{49,33},{2,50}... | collective-permute-start | bytes 344072 | tf_op jit(solution)/shard_map/ppermute | solution.py:302
  23.0 6.9 %collective-permute-start.5 = (bf16[1,224,256]{2,1,0:T(8,128)(2,1)S(1)}, bf16[1,224,256]{2,1,0:T(8,128)(2,1)S(1)}, u32[]{:S(2)}, u32[]{:S(2)}) collective-permute-start(bf16[1,224,256]{2,1,0:T(8,128)(2,1)S(1)} %slice.40), channel_id=1, source_target_pairs={{0,64},{64,128},{128,192},{192,0},{1,65},{65,129},{129,193},{193,1... | collective-permute-start | bytes 344072 | tf_op jit(solution)/shard_map/ppermute | solution.py:302
  23.6 6.3 %collective-permute-start.6 = (bf16[1,224,256]{2,1,0:T(8,128)(2,1)S(1)}, bf16[1,224,256]{2,1,0:T(8,128)(2,1)S(1)}, u32[]{:S(2)}, u32[]{:S(2)}) collective-permute-start(bf16[1,224,256]{2,1,0:T(8,128)(2,1)S(1)} %slice.41), channel_id=1, source_target_pairs={{0,192},{64,0},{128,64},{192,128},{1,193},{65,1},{129,65},{193,129... | collective-permute-start | bytes 344072 | tf_op jit(solution)/shard_map/ppermute | solution.py:302
  27.1 31.5 %collective-permute-start.16 = (bf16[4,2,224,256]{3,2,1,0:T(8,128)(2,1)S(1)}, bf16[4,2,224,256]{3,2,1,0:T(8,128)(2,1)S(1)}, u32[]{:S(2)}, u32[]{:S(2)}) collective-permute-start(bf16[4,2,224,256]{3,2,1,0:T(8,128)(2,1)S(1)} %pad_maximum_fusion.1), channel_id=1, source_target_pairs={{0,64},{64,128},{128,192},{192,0},{1,65},{65,129},{129,193},{193,1... | collective-permute-start | bytes 2752520 | tf_op jit(solution)/shard_map/ppermute | solution.py:300
  28.4 30.3 %collective-permute-start.18 = (bf16[4,2,224,256]{3,2,1,0:T(8,128)(2,1)S(1)}, bf16[4,2,224,256]{3,2,1,0:T(8,128)(2,1)}, u32[]{:S(2)}, u32[]{:S(2)}) collective-permute-start(bf16[4,2,224,256]{3,2,1,0:T(8,128)(2,1)S(1)} %pad_maximum_fusion.1), channel_id=1, source_target_pairs={{0,192},{64,0},{128,64},{192,128},{1,193},{65,1},{129,65},{193,129... | collective-permute-start | bytes 2752520 | tf_op jit(solution)/shard_map/ppermute | solution.py:300
  30.0 32.5 %collective-permute-start.7 = (bf16[4,2,224,256]{3,2,1,0:T(8,128)(2,1)S(1)}, bf16[4,2,224,256]{3,2,1,0:T(8,128)(2,1)}, u32[]{:S(2)}, u32[]{:S(2)}) collective-permute-start(bf16[4,2,224,256]{3,2,1,0:T(8,128)(2,1)S(1)} %pad_maximum_fusion), channel_id=1, source_target_pairs={{0,16},{16,32},{32,48},{48,0},{1,17},{17,33},{33,49},{49,1},{2,18}... | collective-permute-start | bytes 2752520 | tf_op jit(solution)/shard_map/ppermute | solution.py:300
  30.8 32.9 %collective-permute-start.9 = (bf16[4,2,224,256]{3,2,1,0:T(8,128)(2,1)S(1)}, bf16[4,2,224,256]{3,2,1,0:T(8,128)(2,1)}, u32[]{:S(2)}, u32[]{:S(2)}) collective-permute-start(bf16[4,2,224,256]{3,2,1,0:T(8,128)(2,1)S(1)} %pad_maximum_fusion), channel_id=1, source_target_pairs={{0,48},{16,0},{32,16},{48,32},{1,49},{17,1},{33,17},{49,33},{2,50}... | collective-permute-start | bytes 2752520 | tf_op jit(solution)/shard_map/ppermute | solution.py:300
  31.6 8.8 %collective-permute-start.1 = (bf16[224,1024]{1,0:T(8,128)(2,1)}, bf16[224,1024]{1,0:T(8,128)(2,1)}, u32[]{:S(2)}, u32[]{:S(2)}) collective-permute-start(bf16[224,1024]{1,0:T(8,128)(2,1)} %get-tuple-element.19), channel_id=1, source_target_pairs={{0,4},{4,0},{1,5},{5,1},{2,6},{6,2},{3,7},{7,3},{8,12},{12,8},{9,1... | collective-permute-start | bytes 1376264 | tf_op jit(solution)/shard_map/ppermute | solution.py:296
  58.7 26.7 %collective-permute-start.17 = (bf16[2,2,224,256]{3,2,1,0:T(8,128)(2,1)S(1)}, bf16[2,2,224,256]{3,2,1,0:T(8,128)(2,1)S(1)}, u32[]{:S(2)}, u32[]{:S(2)}) collective-permute-start(bf16[2,2,224,256]{3,2,1,0:T(8,128)(2,1)S(1)} %slice.46), channel_id=1, source_target_pairs={{0,64},{64,128},{128,192},{192,0},{1,65},{65,129},{129,193},{193,1... | collective-permute-start | bytes 1376264 | tf_op jit(solution)/shard_map/ppermute | solution.py:302
  59.8 25.5 %collective-permute-start.19 = (bf16[2,2,224,256]{3,2,1,0:T(8,128)(2,1)S(1)}, bf16[2,2,224,256]{3,2,1,0:T(8,128)(2,1)S(1)}, u32[]{:S(2)}, u32[]{:S(2)}) collective-permute-start(bf16[2,2,224,256]{3,2,1,0:T(8,128)(2,1)S(1)} %slice.47), channel_id=1, source_target_pairs={{0,192},{64,0},{128,64},{192,128},{1,193},{65,1},{129,65},{193,129... | collective-permute-start | bytes 1376264 | tf_op jit(solution)/shard_map/ppermute | solution.py:302
  63.6 21.7 %collective-permute-start.8 = (bf16[2,2,224,256]{3,2,1,0:T(8,128)(2,1)S(1)}, bf16[2,2,224,256]{3,2,1,0:T(8,128)(2,1)S(1)}, u32[]{:S(2)}, u32[]{:S(2)}) collective-permute-start(bf16[2,2,224,256]{3,2,1,0:T(8,128)(2,1)S(1)} %slice.42), channel_id=1, source_target_pairs={{0,16},{16,32},{32,48},{48,0},{1,17},{17,33},{33,49},{49,1},{2,18}... | collective-permute-start | bytes 1376264 | tf_op jit(solution)/shard_map/ppermute | solution.py:302
  64.8 20.6 %collective-permute-start.10 = (bf16[2,2,224,256]{3,2,1,0:T(8,128)(2,1)S(1)}, bf16[2,2,224,256]{3,2,1,0:T(8,128)(2,1)S(1)}, u32[]{:S(2)}, u32[]{:S(2)}) collective-permute-start(bf16[2,2,224,256]{3,2,1,0:T(8,128)(2,1)S(1)} %slice.43), channel_id=1, source_target_pairs={{0,48},{16,0},{32,16},{48,32},{1,49},{17,1},{33,17},{49,33},{2,50}... | collective-permute-start | bytes 1376264 | tf_op jit(solution)/shard_map/ppermute | solution.py:302
where the time goes:
time: 138 us; the launch traced here: 137 us
  Pallas kernels  50.7 us (37%)
  blocking collectives  37.9 us (27%)
  starting transfers between devices  24 us (17%)
  waiting for transfers between devices  12.8 us (9%)
  local copies, waits for them, and re-layouts  10.4 us (8%)
    pallas_call x3, Pallas kernels, attention(): pl.pallas_call(functools.partial(kernel, groups=groups, last=last, region...  49.6 us
    all_to_all x1, blocking collectives, whole(): lax.all_to_all(mixed, HEAD + ('zq',), split_axis=0, concat_axis=0, tiled=...  37.9 us
    ppermute x8, starting transfers between devices, ring(): before, after = (lax.ppermute(t, axis, up), lax.ppermute(t, axis, down))  8.58 us
    ppermute x4, starting transfers between devices, ring(): lax.ppermute(after[n:], axis, down)  6.75 us
    ppermute x1, waiting for transfers between devices, whole(): got = lax.ppermute(give, 'zq', swap)  5.91 us
    unnamed x17, local copies, waits for them, and re-layouts  5.32 us
  transfers between devices with their start and end apart: 20, of which 6 were waited for; matrix products, arithmetic and copies ran while one was open for 3% of the time, Pallas kernels for 28%

commit v1 on v0

--- a/solution.py
+++ b/solution.py
@@ -23,19 +23,20 @@
     return [(colour, *h) for g in groups for colour in range(2) for h in RING[g]]
 
 
-def kernel(place_ref, tab_ref, own_ref, got_ref, *refs, groups, last, region, mh):
+def kernel(place_ref, tab_ref, own_ref, got_ref, *refs, groups, last, region, mh, half):
     first = 0 in groups
     homes = homes_of(groups)
     pieces, refs = refs[:len(homes)], refs[len(homes):]
     if not first:
         before, refs = refs[:4], refs[4:]
     if last:
-        out_ref, refs = refs[0], refs[1:]
+        outs, refs = refs[:2], refs[2:]
     m, a, pm, pa, kv, flags, qs, pqs, s0, s1, p0, p1, f0, f1 = refs
     px, py, pp, side = [place_ref[i] for i in range(4)]
     pair = (px * 4 + py) * 2 + pp
     prompts = sum(2 * n * PR for _, _, _, n in homes)
-    per = G // mh
+    nh, h0 = (G, 0) if half is None else (G // 2, half * (G // 2))
+    per = nh // mh
 
     spans = [(place_ref[4 + t], place_ref[6 + t]) for t in range(2)]
     flags[:CH] = jnp.ones((CH, D), jnp.bfloat16)
@@ -75,18 +76,24 @@
     chunks = [(k + CH - 1) // CH for k in keys]
 
     for src, t in ((own_ref, side), (got_ref, 1 - side)):
-        for h in range(G):
-            cols = slice(h * D, (h + 1) * D)
+        for h in range(nh):
+            cols = slice((h0 + h) * D, (h0 + h + 1) * D)
             qs[t * per + h // mh, pl.ds(h % mh * RB, RB)] = src[PR:, cols]
-            pqs[pl.ds((t * G + h) * PR, PR)] = src[:PR, cols]
+            pqs[pl.ds((t * nh + h) * PR, PR)] = src[:PR, cols]
     if first:
         for r in (m, pm):
             r[...] = jnp.full(r.shape, NEG, jnp.float32)
         for r in (a, pa):
             r[...] = jnp.zeros(r.shape, jnp.float32)
-    else:
+    elif half is None:
         for r, b in zip((m, a, pm, pa), before):
             r[...] = b[...]
+    else:
+        for t in range(2):
+            for q in range(per):
+                i, j = t * per + q, (2 * t + half) * per + q
+                m[i], a[i] = before[0][j], before[1][j]
+            pm[t], pa[t] = [b[t, half * nh * PR:(half + 1) * nh * PR] for b in before[2:]]
     for t in range(2):
         def pad(i, c, t=t):
             rows = pl.ds(pl.multiple_of(t * region + i * 64, 64), 64)
@@ -121,10 +128,10 @@
         slot = ((((px + dx) & 3) * 4 + ((py + dy) & 3)) * 2 + (pp ^ colour)) * 2 + (side ^ e)
         where.append(slot * PR + (lane & (PR - 1)))
     where = jnp.concatenate(where, axis=1)
-    half = G * PR
+    asked = nh * PR
     for t in range(2):
-        row = (lax.broadcasted_iota(jnp.int32, (half, 1), 0) & (PR - 1)) + (2 * pair + t) * PR
-        s = jnp.where(where <= row, scores(pqs[t * half:(t + 1) * half], 0, prompts), NEG)
+        row = (lax.broadcasted_iota(jnp.int32, (asked, 1), 0) & (PR - 1)) + (2 * pair + t) * PR
+        s = jnp.where(where <= row, scores(pqs[t * asked:(t + 1) * asked], 0, prompts), NEG)
         p, factor = soft(s, pm, t)
         pa[t] = pa[t] * both(factor) + mixed(p, 0, prompts, jnp.ones((prompts, D), jnp.bfloat16))
 
@@ -175,21 +182,22 @@
     stage_c(total - 1, p1, f1)
 
     if last:
-        parts = out_ref.shape[0] // 2
-        pn, rn = PR // parts, RB // parts
+        zh, n = place_ref[8], 2 * outs[0].shape[0] // 2
+        pn, rn = PR // n, RB // n
         for t in range(2):
-            for h in range(G):
+            for h in range(nh):
                 cols = slice(h * D, (h + 1) * D)
                 i, top = t * per + h // mh, h % mh * RB
-                done = (a[i, top:top + RB, :D] / a[i, top:top + RB, D:]).astype(jnp.bfloat16)
-                rr = slice(h * PR, (h + 1) * PR)
-                asked = (pa[t, rr, :D] / pa[t, rr, D:]).astype(jnp.bfloat16)
-                for d in range(parts):
-                    out_ref[2 * d + t, :pn, cols] = asked[d * pn:(d + 1) * pn]
-                    out_ref[2 * d + t, pn:, cols] = done[d * rn:(d + 1) * rn]
-
-
-def attention(place, table, own, got, pieces, state, groups, parts, mh):
+                for k, out in enumerate(outs):
+                    for core in range(2):
+                        d = 2 * (zh ^ k) + core
+                        rr = pl.ds(pl.multiple_of(h * PR + d * pn, 8), pn)
+                        out[2 * core + t, :pn, cols] = (pa[t, rr, :D] / pa[t, rr, D:]).astype(jnp.bfloat16)
+                        rr = pl.ds(pl.multiple_of(top + d * rn, 8), rn)
+                        out[2 * core + t, pn:, cols] = (a[i, rr, :D] / a[i, rr, D:]).astype(jnp.bfloat16)
+
+
+def attention(place, table, own, got, pieces, state, groups, parts, mh, half=None):
     slots = table.shape[0]
     f32, bf16 = jnp.float32, jnp.bfloat16
     smem = pl.BlockSpec(memory_space=pltpu.SMEM)
@@ -197,18 +205,23 @@
     last = 2 in groups
     count = sum(2 * n for *_, n in homes_of(groups))
     region = -(-(count * PR + min(count, slots // 2) * RB) // CH) * CH
-    units = 2 * G // mh
-    shapes = [(units, mh * RB, D), (units, mh * RB, 2 * D), (2, G * PR, D), (2, G * PR, 2 * D)]
-    state = [x.reshape(shape) for x, shape in zip(state, shapes)]
+
+    def shapes_of(nh):
+        units = 2 * nh // mh
+        return [(units, mh * RB, D), (units, mh * RB, 2 * D), (2, nh * PR, D), (2, nh * PR, 2 * D)]
+
+    nh = G if half is None else G // 2
+    shapes, units = shapes_of(nh), 2 * nh // mh
+    state = [x.reshape(shape) for x, shape in zip(state, shapes_of(G))]
     inputs = [place, table, own, got, *pieces, *state]
     kept = [jax.ShapeDtypeStruct(s, f32) for s in shapes]
     if last:
-        out_shape, out_specs = jax.ShapeDtypeStruct((2 * parts, (PR + RB) // parts, G * D), bf16), vmem
+        out_shape, out_specs = (jax.ShapeDtypeStruct((parts, (PR + RB) // parts, nh * D), bf16),) * 2, (vmem, vmem)
     else:
         out_shape, out_specs = kept, [vmem] * 4
-    flops = 4 * RB * G * 2 * D * (count * (PR + RB // 2))
+    flops = 4 * RB * nh * 2 * D * (count * (PR + RB // 2))
     return pl.pallas_call(
-        functools.partial(kernel, groups=groups, last=last, region=region, mh=mh),
+        functools.partial(kernel, groups=groups, last=last, region=region, mh=mh, half=half),
         out_shape=out_shape,
         in_specs=[smem, smem] + [vmem] * (len(inputs) - 2),
         out_specs=out_specs,
@@ -216,7 +229,7 @@
             pltpu.VMEM((2 * region, 2 * D), bf16),
             pltpu.VMEM((2 * CH, D), bf16),
             pltpu.VMEM((units, mh * RB, D), bf16),
-            pltpu.VMEM((2 * G * PR, D), bf16),
+            pltpu.VMEM((2 * nh * PR, D), bf16),
             pltpu.VMEM((mh * RB, CH), f32), pltpu.VMEM((mh * RB, CH), f32),
             pltpu.VMEM((mh * RB, CH), bf16), pltpu.VMEM((mh * RB, CH), bf16),
             pltpu.VMEM((mh * RB, D), f32), pltpu.VMEM((mh * RB, D), f32),
@@ -232,7 +245,7 @@
     run = functools.partial(attention, place, table, own, got)
     state = run([c[0] for c in gathered], (), (0,), parts, 2)
     state = run([p for c in gathered for p in c[1:3]], state, (1,), parts, 4)
-    return run([p for c in gathered for p in c[3:]], state, (2,), parts, 4)
+    return [run([p for c in gathered for p in c[3:]], state, (2,), parts, 2, half) for half in range(2)]
 
 
 def together(copies):
@@ -274,6 +287,31 @@
     )(side.reshape(1), *arrays)
 
 
+def set_columns(zh_ref, got, prompt_out, answer_out):
+    pn, width = prompt_out.shape[0], got.shape[3]
+    for zh in range(2):
+        @pl.when(zh_ref[0] == zh)
+        def write(zh=zh):
+            for src in range(4):
+                core, zq = src >> 1, src & 1
+                for k in range(2):
+                    block = ((zh ^ k) * 2 + core) * 2 + (zq ^ k)
+                    for half in range(2):
+                        cols = slice((block * 2 + half) * width, (block * 2 + half + 1) * width)
+                        prompt_out[:, cols] = got[src, 2 * k + half, :pn, :]
+                        answer_out[:, cols] = got[src, 2 * k + half, pn:, :]
+
+
+def placed(zh, got, pn):
+    rows, cols = got.shape[2], 16 * got.shape[3]
+    vmem = pl.BlockSpec(memory_space=pltpu.VMEM)
+    return pl.pallas_call(
+        set_columns, out_shape=(jax.ShapeDtypeStruct((pn, cols), jnp.bfloat16), jax.ShapeDtypeStruct((rows - pn, cols), jnp.bfloat16)),
+        in_specs=[pl.BlockSpec(memory_space=pltpu.SMEM), vmem], out_specs=(vmem, vmem),
+        compiler_params=pltpu.CompilerParams(vmem_limit_bytes=16 * 2**20), name="set_columns",
+    )(zh.reshape(1), got)
+
+
 SEQ = ("x", "y", "zp", "zq")
 HEAD = ("zh", "core")
 
@@ -284,7 +322,8 @@
     mates = lax.dynamic_slice_in_dim(table, (place[0] * 4 + place[1]) * 4 + place[2] * 2, 2, 0)
     ends = jnp.cumsum(lengths)
     begun = jnp.where(mates[:, None] >= ends[None, :], ends[None, :], 0)
-    place = jnp.concatenate([jnp.stack(place), mates, jnp.max(begun, axis=1)])
+    zh = lax.axis_index("zh").astype(jnp.int32)
+    place = jnp.concatenate([jnp.stack(place), mates, jnp.max(begun, axis=1), zh.reshape(1)])
     here, there = sorted_by_side(sort_keys, side, (pk, pv, rk, rv), 2 * D)
     keep, give = sorted_by_side(sort_queries, side, (pq, rq), rq.shape[1] // 2)
     swap = [(0, 1), (1, 0)]
@@ -307,11 +346,12 @@
 
     gathered = (colour(jnp.stack([here, next_to]), "x", "y"), colour(jnp.stack([far_same, far_other]), "y", "x"))
     parts = lax.axis_size(HEAD)
-    mixed = attend(place, table, keep, got, gathered, parts)
-    back = lax.all_to_all(mixed, HEAD + ("zq",), split_axis=0, concat_axis=0, tiled=True)
-    pn = PR // parts
-    flat = lambda t: t.transpose(1, 0, 2).reshape(t.shape[1], -1)
-    return flat(back[:, :pn]), flat(back[:, pn:])
+    halves = attend(place, table, keep, got, gathered, parts)
+    cross = [(i, 3 - i) for i in range(4)]
+    moved = [lax.ppermute(h[1], ("zq", "zh"), cross) for h in halves]
+    rest = jnp.stack([halves[0][0], halves[1][0], *moved], axis=1)
+    back = lax.all_to_all(rest, ("core", "zq"), split_axis=0, concat_axis=0, tiled=True)
+    return placed(zh, back, PR // parts)
 
 
 def solution(mesh):

time: 138 us -> 143 us (1.036)
  the two profiles are of different devices: /device:TPU:57 before, /device:TPU:78 now
where the time goes in v1:
time: 143 us
  Pallas kernels  59.3 us (41%)
  starting transfers between devices  31.1 us (22%)
  waiting for transfers between devices  25.6 us (18%)
  blocking collectives  15.4 us (11%)
  local copies, waits for them, and re-layouts  9.73 us (7%)
    pallas_call x4, Pallas kernels, attention(): pl.pallas_call(functools.partial(kernel, groups=groups, last=last, region...  58 us
    all_to_all x1, blocking collectives, whole(): lax.all_to_all(rest, ('core', 'zq'), split_axis=0, concat_axis=0, tiled=T...  15.4 us
    ppermute x2, waiting for transfers between devices, whole(): moved = [lax.ppermute(h[1], ('zq', 'zh'), cross) for h in halves]  9.11 us
    ppermute x8, starting transfers between devices, ring(): before, after = (lax.ppermute(t, axis, up), lax.ppermute(t, axis, down))  8.41 us
    ppermute x2, starting transfers between devices, whole(): moved = [lax.ppermute(h[1], ('zq', 'zh'), cross) for h in halves]  6.14 us
    ppermute x1, waiting for transfers between devices, whole(): got = lax.ppermute(give, 'zq', swap)  5.86 us
    ppermute x4, starting transfers between devices, ring(): lax.ppermute(after[n:], axis, down)  5.57 us
    unnamed x16, local copies, waits for them, and re-layouts  5.26 us
  transfers between devices with their start and end apart: 22, of which 8 were waited for; matrix products, arithmetic and copies ran while one was open for 4% of the time, Pallas kernels for 36%

profile of v1, /device:TPU:78, one launch (start us, length us, event | category | flops | bytes accessed | tf_op | source)
XLA Modules:
  0.0 142.9 jit_solution(14216721086513496872)
XLA Ops:
  0.6 0.9 copy-done.2
  1.5 0.9 copy-done.3
  4.2 4.2 %collective-permute-start.11 = (bf16[224,256]{1,0:T(8,128)(2,1)S(1)}, bf16[224,256]{1,0:T(8,128)(2,1)S(1)}, u32[]{:S(2)}, u32[]{:S(2)}) collective-permute-start(bf16[224,256]{1,0:T(8,128)(2,1)S(1)} %get-tuple-element.24), channel_id=1, source_target_pairs={{0,8},{8,0},{1,9},{9,1},{2,10},{10,2},{3,11},{11,3},{4,12},{12,4},... | collective-permute-start | bytes 344072 | tf_op jit(solution)/shard_map/ppermute | solution.py:331
  8.4 1.1 copy-done
  9.5 0.9 copy-done.1
  10.6 4.3 %collective-permute-done = bf16[224,256]{1,0:T(8,128)(2,1)S(1)} collective-permute-done((bf16[224,256]{1,0:T(8,128)(2,1)S(1)}, bf16[224,256]{1,0:T(8,128)(2,1)S(1)}, u32[]{:S(2)}, u32[]{:S(2)}) %collective-permute-start) | collective-permute-done | bytes 114720 | tf_op jit(solution)/shard_map/ppermute | solution.py:332
  15.0 1.7 %collective-permute-start.13 = (bf16[2,224,256]{2,1,0:T(8,128)(2,1)S(1)}, bf16[2,224,256]{2,1,0:T(8,128)(2,1)S(1)}, u32[]{:S(2)}, u32[]{:S(2)}) collective-permute-start(bf16[2,224,256]{2,1,0:T(8,128)(2,1)S(1)} %get-tuple-element.39), channel_id=1, source_target_pairs={{0,16},{16,32},{32,48},{48,0},{1,17},{17,33},{33,49},{49,1},{2,18}... | collective-permute-start | bytes 688136 | tf_op jit(solution)/shard_map/ppermute | solution.py:339
  17.7 1.5 %collective-permute-start.3 = (bf16[2,224,256]{2,1,0:T(8,128)(2,1)S(1)}, bf16[2,224,256]{2,1,0:T(8,128)(2,1)S(1)}, u32[]{:S(2)}, u32[]{:S(2)}) collective-permute-start(bf16[2,224,256]{2,1,0:T(8,128)(2,1)S(1)} %get-tuple-element.41), channel_id=1, source_target_pairs={{0,192},{64,0},{128,64},{192,128},{1,193},{65,1},{129,65},{193,129... | collective-permute-start | bytes 688136 | tf_op jit(solution)/shard_map/ppermute | solution.py:339
  19.2 1.9 %collective-permute-done.13 = bf16[2,224,256]{2,1,0:T(8,128)(2,1)S(1)} collective-permute-done((bf16[2,224,256]{2,1,0:T(8,128)(2,1)S(1)}, bf16[2,224,256]{2,1,0:T(8,128)(2,1)S(1)}, u32[]{:S(2)}, u32[]{:S(2)}) %collective-permute-start.13) | collective-permute-done | bytes 229408 | tf_op jit(solution)/shard_map/ppermute | solution.py:339
  21.1 1.7 %collective-permute-start.14 = (bf16[1,224,256]{2,1,0:T(8,128)(2,1)S(1)}, bf16[1,224,256]{2,1,0:T(8,128)(2,1)S(1)}, u32[]{:S(2)}, u32[]{:S(2)}) collective-permute-start(bf16[1,224,256]{2,1,0:T(8,128)(2,1)S(1)} %slice.36), channel_id=1, source_target_pairs={{0,16},{16,32},{32,48},{48,0},{1,17},{17,33},{33,49},{49,1},{2,18}... | collective-permute-start | bytes 344072 | tf_op jit(solution)/shard_map/ppermute | solution.py:341
  23.5 1.4 %collective-permute-start.5 = (bf16[1,224,256]{2,1,0:T(8,128)(2,1)S(1)}, bf16[1,224,256]{2,1,0:T(8,128)(2,1)S(1)}, u32[]{:S(2)}, u32[]{:S(2)}) collective-permute-start(bf16[1,224,256]{2,1,0:T(8,128)(2,1)S(1)} %slice.32), channel_id=1, source_target_pairs={{0,64},{64,128},{128,192},{192,0},{1,65},{65,129},{129,193},{193,1... | collective-permute-start | bytes 344072 | tf_op jit(solution)/shard_map/ppermute | solution.py:341
  25.0 0.8 collective-permute-start.6
  26.0 1.7 %collective-permute-done.15 = bf16[1,224,256]{2,1,0:T(8,128)(2,1)S(1)} collective-permute-done((bf16[1,224,256]{2,1,0:T(8,128)(2,1)S(1)}, bf16[1,224,256]{2,1,0:T(8,128)(2,1)S(1)}, u32[]{:S(2)}, u32[]{:S(2)}) %collective-permute-start.15) | collective-permute-done | bytes 114720 | tf_op jit(solution)/shard_map/ppermute | solution.py:341
  28.5 1.4 collective-permute-start.18
  29.9 2.4 %collective-permute-done.6 = bf16[1,224,256]{2,1,0:T(8,128)(2,1)S(1)} collective-permute-done((bf16[1,224,256]{2,1,0:T(8,128)(2,1)S(1)}, bf16[1,224,256]{2,1,0:T(8,128)(2,1)S(1)}, u32[]{:S(2)}, u32[]{:S(2)}) %collective-permute-start.6) | collective-permute-done | bytes 114720 | tf_op jit(solution)/shard_map/ppermute | solution.py:341
  32.4 1.7 %collective-permute-start.7 = (bf16[4,2,224,256]{3,2,1,0:T(8,128)(2,1)S(1)}, bf16[4,2,224,256]{3,2,1,0:T(8,128)(2,1)}, u32[]{:S(2)}, u32[]{:S(2)}) collective-permute-start(bf16[4,2,224,256]{3,2,1,0:T(8,128)(2,1)S(1)} %pad_maximum_fusion), channel_id=1, source_target_pairs={{0,16},{16,32},{32,48},{48,0},{1,17},{17,33},{33,49},{49,1},{2,18}... | collective-permute-start | bytes 2752520 | tf_op jit(solution)/shard_map/ppermute | solution.py:339
  34.6 3.4 %collective-permute-start.1 = (bf16[224,1024]{1,0:T(8,128)(2,1)S(1)}, bf16[224,1024]{1,0:T(8,128)(2,1)S(1)}, u32[]{:S(2)}, u32[]{:S(2)}) collective-permute-start(bf16[224,1024]{1,0:T(8,128)(2,1)S(1)} %get-tuple-element.23), channel_id=1, source_target_pairs={{0,4},{4,0},{1,5},{5,1},{2,6},{6,2},{3,7},{7,3},{8,12},{12,8},{9,1... | collective-permute-start | bytes 1376264 | tf_op jit(solution)/shard_map/ppermute | solution.py:335
  38.5 5.9 %collective-permute-done.1.got_ref = bf16[224,1024]{1,0:T(8,128)(2,1)S(1)} collective-permute-done((bf16[224,1024]{1,0:T(8,128)(2,1)S(1)}, bf16[224,1024]{1,0:T(8,128)(2,1)S(1)}, u32[]{:S(2)}, u32[]{:S(2)}) %collective-permute-start.1) | collective-permute-done | bytes 458784 | tf_op jit(solution)/shard_map/ppermute | solution.py:335
  44.4 14.3 %attention.4 = (f32[8,384,128]{2,1,0:T(8,128)S(1)}, f32[8,384,256]{2,1,0:T(8,128)S(1)}, f32[2,256,128]{2,1,0:T(8,128)S(1)}, f32[2,256,256]{2,1,0:T(8,128)S(1)}) custom-call(s32[9]{0:T(128)S(1)} %concatenate.9.place_ref, s32[64]{0:T(128)S(1)} %copy-done.6, bf16[224,1024]{1,0:T(8,128)(2,1)S(1)} %get-tuple-element.20.own_ref, ...), custom_call_target="tpu_custom_call" | custom-call | flops 3221225472 | bytes 8388608 | tf_op jit(solution)/shard_map/attention/pallas_call | solution.py:223
  58.7 1.0 slice.38
  59.8 1.1 slice.39
  60.9 2.1 %collective-permute-start.19 = (bf16[2,2,224,256]{3,2,1,0:T(8,128)(2,1)S(1)}, bf16[2,2,224,256]{3,2,1,0:T(8,128)(2,1)S(1)}, u32[]{:S(2)}, u32[]{:S(2)}) collective-permute-start(bf16[2,2,224,256]{3,2,1,0:T(8,128)(2,1)S(1)} %slice.39), channel_id=1, source_target_pairs={{0,192},{64,0},{128,64},{192,128},{1,193},{65,1},{129,65},{193,129... | collective-permute-start | bytes 1376264 | tf_op jit(solution)/shard_map/ppermute | solution.py:341
  63.0 1.0 slice.34
  64.1 1.1 slice.35
  65.2 2.1 %collective-permute-start.10 = (bf16[2,2,224,256]{3,2,1,0:T(8,128)(2,1)S(1)}, bf16[2,2,224,256]{3,2,1,0:T(8,128)(2,1)S(1)}, u32[]{:S(2)}, u32[]{:S(2)}) collective-permute-start(bf16[2,2,224,256]{3,2,1,0:T(8,128)(2,1)S(1)} %slice.35), channel_id=1, source_target_pairs={{0,48},{16,0},{32,16},{48,32},{1,49},{17,1},{33,17},{49,33},{2,50}... | collective-permute-start | bytes 1376264 | tf_op jit(solution)/shard_map/ppermute | solution.py:341
  67.3 30.8 %attention.5 = (f32[4,768,128]{2,1,0:T(8,128)S(1)}, f32[4,768,256]{2,1,0:T(8,128)S(1)}, f32[2,256,128]{2,1,0:T(8,128)S(1)}, f32[2,256,256]{2,1,0:T(8,128)S(1)}) custom-call(s32[9]{0:T(128)S(1)} %concatenate.9.place_ref, s32[64]{0:T(128)S(1)} %copy-done.6, bf16[224,1024]{1,0:T(8,128)(2,1)S(1)} %get-tuple-element.20.own_ref, ...), custom_call_target="tpu_custom_call" | custom-call | flops 6442450944 | bytes 8388608 | tf_op jit(solution)/shard_map/attention/pallas_call | solution.py:223
  98.1 6.5 %attention.6 = (bf16[4,56,512]{2,1,0:T(8,128)(2,1)S(1)}, bf16[4,56,512]{2,1,0:T(8,128)(2,1)S(1)}) custom-call(s32[9]{0:T(128)S(1)} %concatenate.9.place_ref, s32[64]{0:T(128)S(1)} %copy-done.6, bf16[224,1024]{1,0:T(8,128)(2,1)S(1)} %get-tuple-element.20.own_ref, bf16[224,1024]{1,0:T(8,128)(2,1)S(1)} %collective-permute-done.1.got_ref, ...), custom_call_target="tpu_custom_call" | custom-call | flops 1610612736 | bytes 8388608 | tf_op jit(solution)/shard_map/attention/pallas_call | solution.py:223
  104.6 6.0 %collective-permute-start.20 = (bf16[4,56,512]{2,1,0:T(8,128)(2,1)S(1)}, bf16[4,56,512]{2,1,0:T(8,128)(2,1)S(1)}, u32[]{:S(2)}, u32[]{:S(2)}) collective-permute-start(bf16[4,56,512]{2,1,0:T(8,128)(2,1)S(1)} %get-tuple-element.36), channel_id=1, source_target_pairs={{0,6},{2,4},{4,2},{6,0},{1,7},{3,5},{5,3},{7,1},{8,14},{10,12},{12... | collective-permute-start | bytes 688136 | tf_op jit(solution)/shard_map/ppermute | solution.py:351
  110.6 6.5 %attention.7 = (bf16[4,56,512]{2,1,0:T(8,128)(2,1)S(1)}, bf16[4,56,512]{2,1,0:T(8,128)(2,1)S(1)}) custom-call(s32[9]{0:T(128)S(1)} %concatenate.9.place_ref, s32[64]{0:T(128)S(1)} %copy-done.6, bf16[224,1024]{1,0:T(8,128)(2,1)S(1)} %get-tuple-element.20.own_ref, bf16[224,1024]{1,0:T(8,128)(2,1)S(1)} %collective-permute-done.1.got_ref, ...), custom_call_target="tpu_custom_call" | custom-call | flops 1610612736 | bytes 8388608 | tf_op jit(solution)/shard_map/attention/pallas_call | solution.py:223
  117.2 9.1 %collective-permute-done.21 = bf16[4,56,512]{2,1,0:T(8,128)(2,1)S(1)} collective-permute-done((bf16[4,56,512]{2,1,0:T(8,128)(2,1)S(1)}, bf16[4,56,512]{2,1,0:T(8,128)(2,1)S(1)}, u32[]{:S(2)}, u32[]{:S(2)}) %collective-permute-start.21) | collective-permute-done | bytes 229408 | tf_op jit(solution)/shard_map/ppermute | solution.py:351
  126.5 15.4 %all_to_all.5.got = bf16[4,4,56,512]{3,2,1,0:T(8,128)(2,1)S(1)} all-to-all(bf16[4,4,56,512]{3,2,1,0:T(8,128)(2,1)S(1)} %pad_maximum_fusion.2), channel_id=1, replica_groups=mesh['x'=4,'y'=4,'zp'=2,'zq'=2,'zh'=2,'core'=2] {'core','zq'}, dimensions={0} | all-to-all | bytes 1835008 | tf_op jit(solution)/shard_map/all_to_all | solution.py:353
  141.9 1.0 set_columns.1
  (57 shorter events, 6.4 us)
Async XLA Ops:
  0.6 0.9 copy-start.2
  1.5 0.9 copy-start.3
  2.4 0.7 copy-start.4
  3.1 0.7 copy-start.5
  4.0 10.9 %collective-permute-start = (bf16[224,256]{1,0:T(8,128)(2,1)S(1)}, bf16[224,256]{1,0:T(8,128)(2,1)S(1)}, u32[]{:S(2)}, u32[]{:S(2)}) collective-permute-start(bf16[224,256]{1,0:T(8,128)(2,1)S(1)} %get-tuple-element.21), channel_id=1, source_target_pairs={{0,12},{4,8},{8,4},{12,0},{1,13},{5,9},{9,5},{13,1},{2,14},{6,10},... | collective-permute-start | bytes 344072 | tf_op jit(solution)/shard_map/ppermute | solution.py:332
  4.2 10.7 %collective-permute-start.11 = (bf16[224,256]{1,0:T(8,128)(2,1)S(1)}, bf16[224,256]{1,0:T(8,128)(2,1)S(1)}, u32[]{:S(2)}, u32[]{:S(2)}) collective-permute-start(bf16[224,256]{1,0:T(8,128)(2,1)S(1)} %get-tuple-element.24), channel_id=1, source_target_pairs={{0,8},{8,0},{1,9},{9,1},{2,10},{10,2},{3,11},{11,3},{4,12},{12,4},... | collective-permute-start | bytes 344072 | tf_op jit(solution)/shard_map/ppermute | solution.py:331
  8.4 8.7 %collective-permute-start.2 = (bf16[224,256]{1,0:T(8,128)(2,1)S(1)}, bf16[224,256]{1,0:T(8,128)(2,1)S(1)}, u32[]{:S(2)}, u32[]{:S(2)}) collective-permute-start(bf16[224,256]{1,0:T(8,128)(2,1)S(1)} %get-tuple-element.21), channel_id=1, source_target_pairs={{0,4},{4,0},{1,5},{5,1},{2,6},{6,2},{3,7},{7,3},{8,12},{12,8},{9,1... | collective-permute-start | bytes 344072 | tf_op jit(solution)/shard_map/ppermute | solution.py:330
  8.4 1.1 copy-start
  9.5 0.9 copy-start.1
  14.9 23.0 %copy-start.7 = (s32[16]{0:T(128)S(1)}, s32[16]{0:T(128)}, u32[]{:S(2)}) copy-start(s32[16]{0:T(128)} %param.14) | copy-start | bytes 196
  14.9 23.2 %copy-start.6 = (s32[64]{0:T(128)S(1)}, s32[64]{0:T(128)}, u32[]{:S(2)}) copy-start(s32[64]{0:T(128)} %tab_ref.7) | copy-start | bytes 772
  15.0 6.2 %collective-permute-start.13 = (bf16[2,224,256]{2,1,0:T(8,128)(2,1)S(1)}, bf16[2,224,256]{2,1,0:T(8,128)(2,1)S(1)}, u32[]{:S(2)}, u32[]{:S(2)}) collective-permute-start(bf16[2,224,256]{2,1,0:T(8,128)(2,1)S(1)} %get-tuple-element.39), channel_id=1, source_target_pairs={{0,16},{16,32},{32,48},{48,0},{1,17},{17,33},{33,49},{49,1},{2,18}... | collective-permute-start | bytes 688136 | tf_op jit(solution)/shard_map/ppermute | solution.py:339
  16.6 6.2 %collective-permute-start.12 = (bf16[2,224,256]{2,1,0:T(8,128)(2,1)S(1)}, bf16[2,224,256]{2,1,0:T(8,128)(2,1)S(1)}, u32[]{:S(2)}, u32[]{:S(2)}) collective-permute-start(bf16[2,224,256]{2,1,0:T(8,128)(2,1)S(1)} %get-tuple-element.39), channel_id=1, source_target_pairs={{0,48},{16,0},{32,16},{48,32},{1,49},{17,1},{33,17},{49,33},{2,50}... | collective-permute-start | bytes 688136 | tf_op jit(solution)/shard_map/ppermute | solution.py:339
  17.1 6.4 %collective-permute-start.4 = (bf16[2,224,256]{2,1,0:T(8,128)(2,1)S(1)}, bf16[2,224,256]{2,1,0:T(8,128)(2,1)S(1)}, u32[]{:S(2)}, u32[]{:S(2)}) collective-permute-start(bf16[2,224,256]{2,1,0:T(8,128)(2,1)S(1)} %get-tuple-element.41), channel_id=1, source_target_pairs={{0,64},{64,128},{128,192},{192,0},{1,65},{65,129},{129,193},{193,1... | collective-permute-start | bytes 688136 | tf_op jit(solution)/shard_map/ppermute | solution.py:339
  17.7 7.3 %collective-permute-start.3 = (bf16[2,224,256]{2,1,0:T(8,128)(2,1)S(1)}, bf16[2,224,256]{2,1,0:T(8,128)(2,1)S(1)}, u32[]{:S(2)}, u32[]{:S(2)}) collective-permute-start(bf16[2,224,256]{2,1,0:T(8,128)(2,1)S(1)} %get-tuple-element.41), channel_id=1, source_target_pairs={{0,192},{64,0},{128,64},{192,128},{1,193},{65,1},{129,65},{193,129... | collective-permute-start | bytes 688136 | tf_op jit(solution)/shard_map/ppermute | solution.py:339
  21.1 4.9 %collective-permute-start.14 = (bf16[1,224,256]{2,1,0:T(8,128)(2,1)S(1)}, bf16[1,224,256]{2,1,0:T(8,128)(2,1)S(1)}, u32[]{:S(2)}, u32[]{:S(2)}) collective-permute-start(bf16[1,224,256]{2,1,0:T(8,128)(2,1)S(1)} %slice.36), channel_id=1, source_target_pairs={{0,16},{16,32},{32,48},{48,0},{1,17},{17,33},{33,49},{49,1},{2,18}... | collective-permute-start | bytes 344072 | tf_op jit(solution)/shard_map/ppermute | solution.py:341
  22.8 4.9 %collective-permute-start.15 = (bf16[1,224,256]{2,1,0:T(8,128)(2,1)S(1)}, bf16[1,224,256]{2,1,0:T(8,128)(2,1)S(1)}, u32[]{:S(2)}, u32[]{:S(2)}) collective-permute-start(bf16[1,224,256]{2,1,0:T(8,128)(2,1)S(1)} %slice.37), channel_id=1, source_target_pairs={{0,48},{16,0},{32,16},{48,32},{1,49},{17,1},{33,17},{49,33},{2,50}... | collective-permute-start | bytes 344072 | tf_op jit(solution)/shard_map/ppermute | solution.py:341
  23.5 6.4 %collective-permute-start.5 = (bf16[1,224,256]{2,1,0:T(8,128)(2,1)S(1)}, bf16[1,224,256]{2,1,0:T(8,128)(2,1)S(1)}, u32[]{:S(2)}, u32[]{:S(2)}) collective-permute-start(bf16[1,224,256]{2,1,0:T(8,128)(2,1)S(1)} %slice.32), channel_id=1, source_target_pairs={{0,64},{64,128},{128,192},{192,0},{1,65},{65,129},{129,193},{193,1... | collective-permute-start | bytes 344072 | tf_op jit(solution)/shard_map/ppermute | solution.py:341
  25.0 7.3 %collective-permute-start.6 = (bf16[1,224,256]{2,1,0:T(8,128)(2,1)S(1)}, bf16[1,224,256]{2,1,0:T(8,128)(2,1)S(1)}, u32[]{:S(2)}, u32[]{:S(2)}) collective-permute-start(bf16[1,224,256]{2,1,0:T(8,128)(2,1)S(1)} %slice.33), channel_id=1, source_target_pairs={{0,192},{64,0},{128,64},{192,128},{1,193},{65,1},{129,65},{193,129... | collective-permute-start | bytes 344072 | tf_op jit(solution)/shard_map/ppermute | solution.py:341
  27.8 30.9 %collective-permute-start.16 = (bf16[4,2,224,256]{3,2,1,0:T(8,128)(2,1)S(1)}, bf16[4,2,224,256]{3,2,1,0:T(8,128)(2,1)}, u32[]{:S(2)}, u32[]{:S(2)}) collective-permute-start(bf16[4,2,224,256]{3,2,1,0:T(8,128)(2,1)S(1)} %pad_maximum_fusion.1), channel_id=1, source_target_pairs={{0,64},{64,128},{128,192},{192,0},{1,65},{65,129},{129,193},{193,1... | collective-permute-start | bytes 2752520 | tf_op jit(solution)/shard_map/ppermute | solution.py:339
  28.5 31.3 %collective-permute-start.18 = (bf16[4,2,224,256]{3,2,1,0:T(8,128)(2,1)S(1)}, bf16[4,2,224,256]{3,2,1,0:T(8,128)(2,1)}, u32[]{:S(2)}, u32[]{:S(2)}) collective-permute-start(bf16[4,2,224,256]{3,2,1,0:T(8,128)(2,1)S(1)} %pad_maximum_fusion.1), channel_id=1, source_target_pairs={{0,192},{64,0},{128,64},{192,128},{1,193},{65,1},{129,65},{193,129... | collective-permute-start | bytes 2752520 | tf_op jit(solution)/shard_map/ppermute | solution.py:339
  32.4 30.5 %collective-permute-start.7 = (bf16[4,2,224,256]{3,2,1,0:T(8,128)(2,1)S(1)}, bf16[4,2,224,256]{3,2,1,0:T(8,128)(2,1)}, u32[]{:S(2)}, u32[]{:S(2)}) collective-permute-start(bf16[4,2,224,256]{3,2,1,0:T(8,128)(2,1)S(1)} %pad_maximum_fusion), channel_id=1, source_target_pairs={{0,16},{16,32},{32,48},{48,0},{1,17},{17,33},{33,49},{49,1},{2,18}... | collective-permute-start | bytes 2752520 | tf_op jit(solution)/shard_map/ppermute | solution.py:339
  34.1 30.0 %collective-permute-start.9 = (bf16[4,2,224,256]{3,2,1,0:T(8,128)(2,1)S(1)}, bf16[4,2,224,256]{3,2,1,0:T(8,128)(2,1)}, u32[]{:S(2)}, u32[]{:S(2)}) collective-permute-start(bf16[4,2,224,256]{3,2,1,0:T(8,128)(2,1)S(1)} %pad_maximum_fusion), channel_id=1, source_target_pairs={{0,48},{16,0},{32,16},{48,32},{1,49},{17,1},{33,17},{49,33},{2,50}... | collective-permute-start | bytes 2752520 | tf_op jit(solution)/shard_map/ppermute | solution.py:339
  34.6 9.8 %collective-permute-start.1 = (bf16[224,1024]{1,0:T(8,128)(2,1)S(1)}, bf16[224,1024]{1,0:T(8,128)(2,1)S(1)}, u32[]{:S(2)}, u32[]{:S(2)}) collective-permute-start(bf16[224,1024]{1,0:T(8,128)(2,1)S(1)} %get-tuple-element.23), channel_id=1, source_target_pairs={{0,4},{4,0},{1,5},{5,1},{2,6},{6,2},{3,7},{7,3},{8,12},{12,8},{9,1... | collective-permute-start | bytes 1376264 | tf_op jit(solution)/shard_map/ppermute | solution.py:335
  59.7 38.3 %collective-permute-start.17 = (bf16[2,2,224,256]{3,2,1,0:T(8,128)(2,1)S(1)}, bf16[2,2,224,256]{3,2,1,0:T(8,128)(2,1)S(1)}, u32[]{:S(2)}, u32[]{:S(2)}) collective-permute-start(bf16[2,2,224,256]{3,2,1,0:T(8,128)(2,1)S(1)} %slice.38), channel_id=1, source_target_pairs={{0,64},{64,128},{128,192},{192,0},{1,65},{65,129},{129,193},{193,1... | collective-permute-start | bytes 1376264 | tf_op jit(solution)/shard_map/ppermute | solution.py:341
  60.9 37.2 %collective-permute-start.19 = (bf16[2,2,224,256]{3,2,1,0:T(8,128)(2,1)S(1)}, bf16[2,2,224,256]{3,2,1,0:T(8,128)(2,1)S(1)}, u32[]{:S(2)}, u32[]{:S(2)}) collective-permute-start(bf16[2,2,224,256]{3,2,1,0:T(8,128)(2,1)S(1)} %slice.39), channel_id=1, source_target_pairs={{0,192},{64,0},{128,64},{192,128},{1,193},{65,1},{129,65},{193,129... | collective-permute-start | bytes 1376264 | tf_op jit(solution)/shard_map/ppermute | solution.py:341
  64.0 34.1 %collective-permute-start.8 = (bf16[2,2,224,256]{3,2,1,0:T(8,128)(2,1)S(1)}, bf16[2,2,224,256]{3,2,1,0:T(8,128)(2,1)S(1)}, u32[]{:S(2)}, u32[]{:S(2)}) collective-permute-start(bf16[2,2,224,256]{3,2,1,0:T(8,128)(2,1)S(1)} %slice.34), channel_id=1, source_target_pairs={{0,16},{16,32},{32,48},{48,0},{1,17},{17,33},{33,49},{49,1},{2,18}... | collective-permute-start | bytes 1376264 | tf_op jit(solution)/shard_map/ppermute | solution.py:341
  65.2 32.9 %collective-permute-start.10 = (bf16[2,2,224,256]{3,2,1,0:T(8,128)(2,1)S(1)}, bf16[2,2,224,256]{3,2,1,0:T(8,128)(2,1)S(1)}, u32[]{:S(2)}, u32[]{:S(2)}) collective-permute-start(bf16[2,2,224,256]{3,2,1,0:T(8,128)(2,1)S(1)} %slice.35), channel_id=1, source_target_pairs={{0,48},{16,0},{32,16},{48,32},{1,49},{17,1},{33,17},{49,33},{2,50}... | collective-permute-start | bytes 1376264 | tf_op jit(solution)/shard_map/ppermute | solution.py:341
  104.6 12.6 %collective-permute-start.20 = (bf16[4,56,512]{2,1,0:T(8,128)(2,1)S(1)}, bf16[4,56,512]{2,1,0:T(8,128)(2,1)S(1)}, u32[]{:S(2)}, u32[]{:S(2)}) collective-permute-start(bf16[4,56,512]{2,1,0:T(8,128)(2,1)S(1)} %get-tuple-element.36), channel_id=1, source_target_pairs={{0,6},{2,4},{4,2},{6,0},{1,7},{3,5},{5,3},{7,1},{8,14},{10,12},{12... | collective-permute-start | bytes 688136 | tf_op jit(solution)/shard_map/ppermute | solution.py:351
  117.1 9.2 %collective-permute-start.21 = (bf16[4,56,512]{2,1,0:T(8,128)(2,1)S(1)}, bf16[4,56,512]{2,1,0:T(8,128)(2,1)S(1)}, u32[]{:S(2)}, u32[]{:S(2)}) collective-permute-start(bf16[4,56,512]{2,1,0:T(8,128)(2,1)S(1)} %get-tuple-element.37), channel_id=1, source_target_pairs={{0,6},{2,4},{4,2},{6,0},{1,7},{3,5},{5,3},{7,1},{8,14},{10,12},{12... | collective-permute-start | bytes 688136 | tf_op jit(solution)/shard_map/ppermute | solution.py:351

commit v2 on v1

--- a/solution.py
+++ b/solution.py
@@ -16,7 +16,7 @@
 LIMIT = 36 * 2**20
 PER_EXP = 128 ** -0.5 * 1.4426950408889634
 NEG = -1e30
-RING = (((0, 0, 4),), ((3, 0, 4), (1, 0, 4)), ((2, 0, 2), (2, 2, 2)))
+RING = (((0, 0, 4),), ((3, 0, 4), (1, 0, 4)), ((2, 0, 4),))
 
 
 def homes_of(groups):
@@ -33,6 +33,7 @@
         outs, refs = refs[:2], refs[2:]
     m, a, pm, pa, kv, flags, qs, pqs, s0, s1, p0, p1, f0, f1 = refs
     px, py, pp, side = [place_ref[i] for i in range(4)]
+    turn = 1 - 2 * place_ref[9]
     pair = (px * 4 + py) * 2 + pp
     prompts = sum(2 * n * PR for _, _, _, n in homes)
     nh, h0 = (G, 0) if half is None else (G // 2, half * (G // 2))
@@ -51,7 +52,7 @@
         def bring(i, counts, piece=piece, colour=colour, far=far, lead=lead, at=at):
             near, e = i >> 1, i & 1
             dx, dy = (lead + near, far) if colour == 0 else (far, lead + near)
-            slot = ((((px + dx) & 3) * 4 + ((py + dy) & 3)) * 2 + (pp ^ colour)) * 2 + (side ^ e)
+            slot = ((((px + turn * dx) & 3) * 4 + ((py + turn * dy) & 3)) * 2 + (pp ^ colour)) * 2 + (side ^ e)
             g = tab_ref[slot]
             new = []
             for t in range(2):
@@ -125,7 +126,7 @@
         lane = lax.broadcasted_iota(jnp.int32, (1, 2 * n * PR), 1)
         near, e = lead + (lane >> 6), (lane >> 5) & 1
         dx, dy = (near, jnp.int32(far)) if colour == 0 else (jnp.int32(far), near)
-        slot = ((((px + dx) & 3) * 4 + ((py + dy) & 3)) * 2 + (pp ^ colour)) * 2 + (side ^ e)
+        slot = ((((px + turn * dx) & 3) * 4 + ((py + turn * dy) & 3)) * 2 + (pp ^ colour)) * 2 + (side ^ e)
         where.append(slot * PR + (lane & (PR - 1)))
     where = jnp.concatenate(where, axis=1)
     asked = nh * PR
@@ -323,7 +324,8 @@
     ends = jnp.cumsum(lengths)
     begun = jnp.where(mates[:, None] >= ends[None, :], ends[None, :], 0)
     zh = lax.axis_index("zh").astype(jnp.int32)
-    place = jnp.concatenate([jnp.stack(place), mates, jnp.max(begun, axis=1), zh.reshape(1)])
+    place = jnp.concatenate([jnp.stack(place), mates, jnp.max(begun, axis=1), zh.reshape(1),
+                             lax.axis_index("core").astype(jnp.int32).reshape(1)])
     here, there = sorted_by_side(sort_keys, side, (pk, pv, rk, rv), 2 * D)
     keep, give = sorted_by_side(sort_queries, side, (pq, rq), rq.shape[1] // 2)
     swap = [(0, 1), (1, 0)]
@@ -335,14 +337,15 @@
     got = lax.ppermute(give, "zq", swap)
 
     def ring(t, axis):
-        up, down = [(i, (i + 1) % 4) for i in range(4)], [(i, (i - 1) % 4) for i in range(4)]
-        before, after = lax.ppermute(t, axis, up), lax.ppermute(t, axis, down)
-        n = t.shape[0] // 2
-        return t, before, after, lax.ppermute(before[:n], axis, up), lax.ppermute(after[n:], axis, down)
+        ahead = [(2 * i + c, (i + 1 - 2 * c) % 4 * 2 + c) for i in range(4) for c in range(2)]
+        astern = [(b, a) for a, b in ahead]
+        first = lax.ppermute(t, (axis, "core"), ahead)
+        second = lax.ppermute(t, (axis, "core"), astern)
+        return t, first, second, lax.ppermute(first, (axis, "core"), ahead)
 
     def colour(t, first, second):
-        own, before, after, half_a, half_b = ring(t, first)
-        return ring(jnp.stack([own, after, jnp.concatenate([half_a, half_b], axis=0), before]), second)
+        own, before, after, far = ring(t, first)
+        return ring(jnp.stack([own, after, far, before]), second)
 
     gathered = (colour(jnp.stack([here, next_to]), "x", "y"), colour(jnp.stack([far_same, far_other]), "y", "x"))
     parts = lax.axis_size(HEAD)

time: 143 us -> 149 us (1.042)
  waiting for transfers between devices: 25.6 us -> 35.9 us
  local copies, waits for them, and re-layouts: 9.73 us -> 5.5 us
  starting transfers between devices: 31.1 us -> 27.6 us
  other arithmetic: 0.8 us -> 2.62 us
    ppermute x16 -> x12, waiting for transfers between devices: 6.29 us -> 22.5 us  [the longest x4 19.5 us: ring(): first = lax.ppermute(t, (axis, 'core'), ahead)]
    ppermute x1, waiting for transfers between devices: 5.86 us -> 0.01 us  [whole(): got = lax.ppermute(give, 'zq', swap)]
    slice x8 -> x0, local copies, waits for them, and re-layouts: 4.23 us -> none  [the longest x4 2.12 us: ring(): after[n:]]
    ppermute x16 -> x12, starting transfers between devices: 17.3 us -> 13.7 us  [the longest x4 6.43 us: ring(): return (t, first, second, lax.ppermute(first, (axis, 'core'), ahead))]
    another operation x8 -> x6, other arithmetic: 0.5 us -> 2.32 us  [the longest x4 2.16 us: colour(): return ring(jnp.stack([own, after, far, before]), second)]
  transfers between devices with their start and end apart: 22 -> 18, of which waited for: 8 -> 6; matrix products, arithmetic and copies ran while one was open for 4% -> 2% of each run, Pallas kernels for 36% -> 36%
where the time goes in v2:
time: 149 us; the launch traced here: 148 us
  Pallas kernels  60.3 us (40%)
  waiting for transfers between devices  35.9 us (24%)
  starting transfers between devices  27.6 us (19%)
  blocking collectives  15.4 us (10%)
  local copies, waits for them, and re-layouts  5.5 us (4%)
  other arithmetic  2.62 us (2%)
    pallas_call x4, Pallas kernels, attention(): pl.pallas_call(functools.partial(kernel, groups=groups, last=last, region...  59 us
    ppermute x4, waiting for transfers between devices, ring(): first = lax.ppermute(t, (axis, 'core'), ahead)  19.5 us
    all_to_all x1, blocking collectives, whole(): lax.all_to_all(rest, ('core', 'zq'), split_axis=0, concat_axis=0, tiled=T...  15.4 us
    ppermute x2, waiting for transfers between devices, whole(): moved = [lax.ppermute(h[1], ('zq', 'zh'), cross) for h in halves]  9.1 us
    ppermute x2, starting transfers between devices, whole(): moved = [lax.ppermute(h[1], ('zq', 'zh'), cross) for h in halves]  6.89 us
    ppermute x4, starting transfers between devices, ring(): return (t, first, second, lax.ppermute(first, (axis, 'core'), ahead))  6.43 us
    unnamed x16, local copies, waits for them, and re-layouts  5.26 us
    ppermute x1, waiting for transfers between devices, whole(): lax.ppermute(there, ('zp', 'zq'), [(i, 3 - i) for i in range(4)])  4.33 us
  transfers between devices with their start and end apart: 18, of which 6 were waited for; matrix products, arithmetic and copies ran while one was open for 2% of the time, Pallas kernels for 36%

profile of v2, /device:TPU:78, one launch (start us, length us, event | category | flops | bytes accessed | tf_op | source)
XLA Modules:
  0.0 148.2 jit_solution(1423675559350829578)
XLA Ops:
  0.7 0.9 copy-done.2
  1.5 0.9 copy-done.3
  2.4 0.7 copy-done.4
  3.2 0.7 copy-done.5
  4.2 4.2 %collective-permute-start.8 = (bf16[224,256]{1,0:T(8,128)(2,1)S(1)}, bf16[224,256]{1,0:T(8,128)(2,1)S(1)}, u32[]{:S(2)}, u32[]{:S(2)}) collective-permute-start(bf16[224,256]{1,0:T(8,128)(2,1)S(1)} %get-tuple-element.24), channel_id=1, source_target_pairs={{0,8},{8,0},{1,9},{9,1},{2,10},{10,2},{3,11},{11,3},{4,12},{12,4},... | collective-permute-start | bytes 344072 | tf_op jit(solution)/shard_map/ppermute | solution.py:333
  8.4 1.1 copy-done
  9.5 0.9 copy-done.1
  10.6 4.3 %collective-permute-done = bf16[224,256]{1,0:T(8,128)(2,1)S(1)} collective-permute-done((bf16[224,256]{1,0:T(8,128)(2,1)S(1)}, bf16[224,256]{1,0:T(8,128)(2,1)S(1)}, u32[]{:S(2)}, u32[]{:S(2)}) %collective-permute-start) | collective-permute-done | bytes 114720 | tf_op jit(solution)/shard_map/ppermute | solution.py:334
  14.9 1.7 %collective-permute-start.10 = (bf16[2,224,256]{2,1,0:T(8,128)(2,1)S(1)}, bf16[2,224,256]{2,1,0:T(8,128)(2,1)S(1)}, u32[]{:S(2)}, u32[]{:S(2)}) collective-permute-start(bf16[2,224,256]{2,1,0:T(8,128)(2,1)S(1)} %get-tuple-element.39), channel_id=1, source_target_pairs={{0,16},{1,49},{16,32},{17,1},{32,48},{33,17},{48,0},{49,33},{2,18}... | collective-permute-start | bytes 688136 | tf_op jit(solution)/shard_map/ppermute | solution.py:342
  16.6 0.6 collective-permute-start.4
  17.2 0.5 collective-permute-start.9
  17.6 5.4 %collective-permute-done.10 = bf16[2,224,256]{2,1,0:T(8,128)(2,1)S(1)} collective-permute-done((bf16[2,224,256]{2,1,0:T(8,128)(2,1)S(1)}, bf16[2,224,256]{2,1,0:T(8,128)(2,1)S(1)}, u32[]{:S(2)}, u32[]{:S(2)}) %collective-permute-start.10) | collective-permute-done | bytes 229408 | tf_op jit(solution)/shard_map/ppermute | solution.py:342
  23.4 0.5 collective-permute-start.3
  23.9 2.7 %collective-permute-start.5 = (bf16[2,224,256]{2,1,0:T(8,128)(2,1)S(1)}, bf16[2,224,256]{2,1,0:T(8,128)(2,1)S(1)}, u32[]{:S(2)}, u32[]{:S(2)}) collective-permute-start(bf16[2,224,256]{2,1,0:T(8,128)(2,1)S(1)} %collective-permute-done.4), channel_id=1, source_target_pairs={{0,64},{1,193},{64,128},{65,1},{128,192},{129,65},{192,0},{193,129... | collective-permute-start | bytes 688136 | tf_op jit(solution)/shard_map/ppermute | solution.py:344
  26.6 2.5 %collective-permute-done.11 = bf16[2,224,256]{2,1,0:T(8,128)(2,1)S(1)} collective-permute-done((bf16[2,224,256]{2,1,0:T(8,128)(2,1)S(1)}, bf16[2,224,256]{2,1,0:T(8,128)(2,1)S(1)}, u32[]{:S(2)}, u32[]{:S(2)}) %collective-permute-start.11) | collective-permute-done | bytes 229408 | tf_op jit(solution)/shard_map/ppermute | solution.py:344
  29.1 1.1 pad_maximum_fusion.1
  30.1 0.5 collective-permute-done.3
  30.6 1.0 pad_maximum_fusion
  31.6 1.8 %collective-permute-start.6 = (bf16[4,2,224,256]{3,2,1,0:T(8,128)(2,1)}, bf16[4,2,224,256]{3,2,1,0:T(8,128)(2,1)}, u32[]{:S(2)}, u32[]{:S(2)}) collective-permute-start(bf16[4,2,224,256]{3,2,1,0:T(8,128)(2,1)} %pad_maximum_fusion), channel_id=1, source_target_pairs={{0,16},{1,49},{16,32},{17,1},{32,48},{33,17},{48,0},{49,33},{2,18}... | collective-permute-start | bytes 2752520 | tf_op jit(solution)/shard_map/ppermute | solution.py:342
  33.5 2.2 %collective-permute-start.14 = (bf16[4,2,224,256]{3,2,1,0:T(8,128)(2,1)}, bf16[4,2,224,256]{3,2,1,0:T(8,128)(2,1)}, u32[]{:S(2)}, u32[]{:S(2)}) collective-permute-start(bf16[4,2,224,256]{3,2,1,0:T(8,128)(2,1)} %pad_maximum_fusion), channel_id=1, source_target_pairs={{16,0},{49,1},{32,16},{1,17},{48,32},{17,33},{0,48},{33,49},{18,2}... | collective-permute-start | bytes 2752520 | tf_op jit(solution)/shard_map/ppermute | solution.py:343
  35.7 2.7 %collective-permute-start.1 = (bf16[224,1024]{1,0:T(8,128)(2,1)S(1)}, bf16[224,1024]{1,0:T(8,128)(2,1)S(1)}, u32[]{:S(2)}, u32[]{:S(2)}) collective-permute-start(bf16[224,1024]{1,0:T(8,128)(2,1)S(1)} %get-tuple-element.23), channel_id=1, source_target_pairs={{0,4},{4,0},{1,5},{5,1},{2,6},{6,2},{3,7},{7,3},{8,12},{12,8},{9,1... | collective-permute-start | bytes 1376264 | tf_op jit(solution)/shard_map/ppermute | solution.py:337
  38.7 14.1 %collective-permute-done.12 = bf16[4,2,224,256]{3,2,1,0:T(8,128)(2,1)} collective-permute-done((bf16[4,2,224,256]{3,2,1,0:T(8,128)(2,1)}, bf16[4,2,224,256]{3,2,1,0:T(8,128)(2,1)}, u32[]{:S(2)}, u32[]{:S(2)}) %collective-permute-start.12) | collective-permute-done | bytes 917536 | tf_op jit(solution)/shard_map/ppermute | solution.py:342
  52.8 1.9 %collective-permute-start.13 = (bf16[4,2,224,256]{3,2,1,0:T(8,128)(2,1)}, bf16[4,2,224,256]{3,2,1,0:T(8,128)(2,1)S(1)}, u32[]{:S(2)}, u32[]{:S(2)}) collective-permute-start(bf16[4,2,224,256]{3,2,1,0:T(8,128)(2,1)} %collective-permute-done.12), channel_id=1, source_target_pairs={{0,64},{1,193},{64,128},{65,1},{128,192},{129,65},{192,0},{193,129... | collective-permute-start | bytes 2752520 | tf_op jit(solution)/shard_map/ppermute | solution.py:344
  54.7 1.6 %collective-permute-start.7 = (bf16[4,2,224,256]{3,2,1,0:T(8,128)(2,1)}, bf16[4,2,224,256]{3,2,1,0:T(8,128)(2,1)S(1)}, u32[]{:S(2)}, u32[]{:S(2)}) collective-permute-start(bf16[4,2,224,256]{3,2,1,0:T(8,128)(2,1)} %collective-permute-done.6), channel_id=1, source_target_pairs={{0,16},{1,49},{16,32},{17,1},{32,48},{33,17},{48,0},{49,33},{2,18}... | collective-permute-start | bytes 2752520 | tf_op jit(solution)/shard_map/ppermute | solution.py:344
  56.5 15.2 %attention.4 = (f32[8,384,128]{2,1,0:T(8,128)S(1)}, f32[8,384,256]{2,1,0:T(8,128)S(1)}, f32[2,256,128]{2,1,0:T(8,128)S(1)}, f32[2,256,256]{2,1,0:T(8,128)S(1)}) custom-call(s32[10]{0:T(128)S(1)} %concatenate.3.place_ref, s32[64]{0:T(128)S(1)} %copy-done.6, bf16[224,1024]{1,0:T(8,128)(2,1)S(1)} %get-tuple-element.20.own_ref, ...), custom_call_target="tpu_custom_call" | custom-call | flops 3221225472 | bytes 8388608 | tf_op jit(solution)/shard_map/attention/pallas_call | solution.py:224
  71.8 30.8 %attention.5 = (f32[4,768,128]{2,1,0:T(8,128)S(1)}, f32[4,768,256]{2,1,0:T(8,128)S(1)}, f32[2,256,128]{2,1,0:T(8,128)S(1)}, f32[2,256,256]{2,1,0:T(8,128)S(1)}) custom-call(s32[10]{0:T(128)S(1)} %concatenate.3.place_ref, s32[64]{0:T(128)S(1)} %copy-done.6, bf16[224,1024]{1,0:T(8,128)(2,1)S(1)} %get-tuple-element.20.own_ref, ...), custom_call_target="tpu_custom_call" | custom-call | flops 6442450944 | bytes 8388608 | tf_op jit(solution)/shard_map/attention/pallas_call | solution.py:224
  102.7 6.5 %attention.6 = (bf16[4,56,512]{2,1,0:T(8,128)(2,1)S(1)}, bf16[4,56,512]{2,1,0:T(8,128)(2,1)S(1)}) custom-call(s32[10]{0:T(128)S(1)} %concatenate.3.place_ref, s32[64]{0:T(128)S(1)} %copy-done.6, bf16[224,1024]{1,0:T(8,128)(2,1)S(1)} %get-tuple-element.20.own_ref, bf16[224,1024]{1,0:T(8,128)(2,1)S(1)} %collective-permute-done.1.got_ref, ...), custom_call_target="tpu_custom_call" | custom-call | flops 1610612736 | bytes 8388608 | tf_op jit(solution)/shard_map/attention/pallas_call | solution.py:224
  109.2 6.8 %collective-permute-start.16 = (bf16[4,56,512]{2,1,0:T(8,128)(2,1)S(1)}, bf16[4,56,512]{2,1,0:T(8,128)(2,1)S(1)}, u32[]{:S(2)}, u32[]{:S(2)}) collective-permute-start(bf16[4,56,512]{2,1,0:T(8,128)(2,1)S(1)} %get-tuple-element.36), channel_id=1, source_target_pairs={{0,6},{2,4},{4,2},{6,0},{1,7},{3,5},{5,3},{7,1},{8,14},{10,12},{12... | collective-permute-start | bytes 688136 | tf_op jit(solution)/shard_map/ppermute | solution.py:354
  115.9 6.5 %attention.7 = (bf16[4,56,512]{2,1,0:T(8,128)(2,1)S(1)}, bf16[4,56,512]{2,1,0:T(8,128)(2,1)S(1)}) custom-call(s32[10]{0:T(128)S(1)} %concatenate.3.place_ref, s32[64]{0:T(128)S(1)} %copy-done.6, bf16[224,1024]{1,0:T(8,128)(2,1)S(1)} %get-tuple-element.20.own_ref, bf16[224,1024]{1,0:T(8,128)(2,1)S(1)} %collective-permute-done.1.got_ref, ...), custom_call_target="tpu_custom_call" | custom-call | flops 1610612736 | bytes 8388608 | tf_op jit(solution)/shard_map/attention/pallas_call | solution.py:224
  122.5 9.1 %collective-permute-done.17 = bf16[4,56,512]{2,1,0:T(8,128)(2,1)S(1)} collective-permute-done((bf16[4,56,512]{2,1,0:T(8,128)(2,1)S(1)}, bf16[4,56,512]{2,1,0:T(8,128)(2,1)S(1)}, u32[]{:S(2)}, u32[]{:S(2)}) %collective-permute-start.17) | collective-permute-done | bytes 229408 | tf_op jit(solution)/shard_map/ppermute | solution.py:354
  131.8 15.4 %all_to_all.5.got = bf16[4,4,56,512]{3,2,1,0:T(8,128)(2,1)S(1)} all-to-all(bf16[4,4,56,512]{3,2,1,0:T(8,128)(2,1)S(1)} %pad_maximum_fusion.2), channel_id=1, replica_groups=mesh['x'=4,'y'=4,'zp'=2,'zq'=2,'zh'=2,'core'=2] {'core','zq'}, dimensions={0} | all-to-all | bytes 1835008 | tf_op jit(solution)/shard_map/all_to_all | solution.py:356
  147.2 1.0 set_columns.1
  (39 shorter events, 1.7 us)
Async XLA Ops:
  0.6 37.7 %copy-start.7 = (s32[16]{0:T(128)S(1)}, s32[16]{0:T(128)}, u32[]{:S(2)}) copy-start(s32[16]{0:T(128)} %param.14) | copy-start | bytes 196
  0.6 0.9 copy-start.2
  1.5 0.9 copy-start.3
  2.4 0.7 copy-start.4
  3.2 0.7 copy-start.5
  3.9 34.7 %copy-start.6 = (s32[64]{0:T(128)S(1)}, s32[64]{0:T(128)}, u32[]{:S(2)}) copy-start(s32[64]{0:T(128)} %tab_ref.7) | copy-start | bytes 772
  4.0 10.9 %collective-permute-start = (bf16[224,256]{1,0:T(8,128)(2,1)S(1)}, bf16[224,256]{1,0:T(8,128)(2,1)S(1)}, u32[]{:S(2)}, u32[]{:S(2)}) collective-permute-start(bf16[224,256]{1,0:T(8,128)(2,1)S(1)} %get-tuple-element.21), channel_id=1, source_target_pairs={{0,12},{4,8},{8,4},{12,0},{1,13},{5,9},{9,5},{13,1},{2,14},{6,10},... | collective-permute-start | bytes 344072 | tf_op jit(solution)/shard_map/ppermute | solution.py:334
  4.2 10.7 %collective-permute-start.8 = (bf16[224,256]{1,0:T(8,128)(2,1)S(1)}, bf16[224,256]{1,0:T(8,128)(2,1)S(1)}, u32[]{:S(2)}, u32[]{:S(2)}) collective-permute-start(bf16[224,256]{1,0:T(8,128)(2,1)S(1)} %get-tuple-element.24), channel_id=1, source_target_pairs={{0,8},{8,0},{1,9},{9,1},{2,10},{10,2},{3,11},{11,3},{4,12},{12,4},... | collective-permute-start | bytes 344072 | tf_op jit(solution)/shard_map/ppermute | solution.py:333
  8.4 8.2 %collective-permute-start.2 = (bf16[224,256]{1,0:T(8,128)(2,1)S(1)}, bf16[224,256]{1,0:T(8,128)(2,1)S(1)}, u32[]{:S(2)}, u32[]{:S(2)}) collective-permute-start(bf16[224,256]{1,0:T(8,128)(2,1)S(1)} %get-tuple-element.21), channel_id=1, source_target_pairs={{0,4},{4,0},{1,5},{5,1},{2,6},{6,2},{3,7},{7,3},{8,12},{12,8},{9,1... | collective-permute-start | bytes 344072 | tf_op jit(solution)/shard_map/ppermute | solution.py:332
  8.4 1.1 copy-start
  9.5 0.9 copy-start.1
  14.9 8.1 %collective-permute-start.10 = (bf16[2,224,256]{2,1,0:T(8,128)(2,1)S(1)}, bf16[2,224,256]{2,1,0:T(8,128)(2,1)S(1)}, u32[]{:S(2)}, u32[]{:S(2)}) collective-permute-start(bf16[2,224,256]{2,1,0:T(8,128)(2,1)S(1)} %get-tuple-element.39), channel_id=1, source_target_pairs={{0,16},{1,49},{16,32},{17,1},{32,48},{33,17},{48,0},{49,33},{2,18}... | collective-permute-start | bytes 688136 | tf_op jit(solution)/shard_map/ppermute | solution.py:342
  16.6 7.3 %collective-permute-start.4 = (bf16[2,224,256]{2,1,0:T(8,128)(2,1)S(1)}, bf16[2,224,256]{2,1,0:T(8,128)(2,1)S(1)}, u32[]{:S(2)}, u32[]{:S(2)}) collective-permute-start(bf16[2,224,256]{2,1,0:T(8,128)(2,1)S(1)} %get-tuple-element.41), channel_id=1, source_target_pairs={{0,64},{1,193},{64,128},{65,1},{128,192},{129,65},{192,0},{193,129... | collective-permute-start | bytes 688136 | tf_op jit(solution)/shard_map/ppermute | solution.py:342
  17.2 9.4 %collective-permute-start.9 = (bf16[2,224,256]{2,1,0:T(8,128)(2,1)S(1)}, bf16[2,224,256]{2,1,0:T(8,128)(2,1)S(1)}, u32[]{:S(2)}, u32[]{:S(2)}) collective-permute-start(bf16[2,224,256]{2,1,0:T(8,128)(2,1)S(1)} %get-tuple-element.39), channel_id=1, source_target_pairs={{16,0},{49,1},{32,16},{1,17},{48,32},{17,33},{0,48},{33,49},{18,2}... | collective-permute-start | bytes 688136 | tf_op jit(solution)/shard_map/ppermute | solution.py:343
  23.0 6.0 %collective-permute-start.11 = (bf16[2,224,256]{2,1,0:T(8,128)(2,1)S(1)}, bf16[2,224,256]{2,1,0:T(8,128)(2,1)S(1)}, u32[]{:S(2)}, u32[]{:S(2)}) collective-permute-start(bf16[2,224,256]{2,1,0:T(8,128)(2,1)S(1)} %collective-permute-done.10), channel_id=1, source_target_pairs={{0,16},{1,49},{16,32},{17,1},{32,48},{33,17},{48,0},{49,33},{2,18}... | collective-permute-start | bytes 688136 | tf_op jit(solution)/shard_map/ppermute | solution.py:344
  23.4 7.2 %collective-permute-start.3 = (bf16[2,224,256]{2,1,0:T(8,128)(2,1)S(1)}, bf16[2,224,256]{2,1,0:T(8,128)(2,1)S(1)}, u32[]{:S(2)}, u32[]{:S(2)}) collective-permute-start(bf16[2,224,256]{2,1,0:T(8,128)(2,1)S(1)} %get-tuple-element.41), channel_id=1, source_target_pairs={{64,0},{193,1},{128,64},{1,65},{192,128},{65,129},{0,192},{129,193... | collective-permute-start | bytes 688136 | tf_op jit(solution)/shard_map/ppermute | solution.py:343
  23.9 6.7 %collective-permute-start.5 = (bf16[2,224,256]{2,1,0:T(8,128)(2,1)S(1)}, bf16[2,224,256]{2,1,0:T(8,128)(2,1)S(1)}, u32[]{:S(2)}, u32[]{:S(2)}) collective-permute-start(bf16[2,224,256]{2,1,0:T(8,128)(2,1)S(1)} %collective-permute-done.4), channel_id=1, source_target_pairs={{0,64},{1,193},{64,128},{65,1},{128,192},{129,65},{192,0},{193,129... | collective-permute-start | bytes 688136 | tf_op jit(solution)/shard_map/ppermute | solution.py:344
  30.1 22.7 %collective-permute-start.12 = (bf16[4,2,224,256]{3,2,1,0:T(8,128)(2,1)}, bf16[4,2,224,256]{3,2,1,0:T(8,128)(2,1)}, u32[]{:S(2)}, u32[]{:S(2)}) collective-permute-start(bf16[4,2,224,256]{3,2,1,0:T(8,128)(2,1)} %pad_maximum_fusion.1), channel_id=1, source_target_pairs={{0,64},{1,193},{64,128},{65,1},{128,192},{129,65},{192,0},{193,129... | collective-permute-start | bytes 2752520 | tf_op jit(solution)/shard_map/ppermute | solution.py:342
  31.6 23.1 %collective-permute-start.6 = (bf16[4,2,224,256]{3,2,1,0:T(8,128)(2,1)}, bf16[4,2,224,256]{3,2,1,0:T(8,128)(2,1)}, u32[]{:S(2)}, u32[]{:S(2)}) collective-permute-start(bf16[4,2,224,256]{3,2,1,0:T(8,128)(2,1)} %pad_maximum_fusion), channel_id=1, source_target_pairs={{0,16},{1,49},{16,32},{17,1},{32,48},{33,17},{48,0},{49,33},{2,18}... | collective-permute-start | bytes 2752520 | tf_op jit(solution)/shard_map/ppermute | solution.py:342
  33.5 38.3 %collective-permute-start.15 = (bf16[4,2,224,256]{3,2,1,0:T(8,128)(2,1)}, bf16[4,2,224,256]{3,2,1,0:T(8,128)(2,1)}, u32[]{:S(2)}, u32[]{:S(2)}) collective-permute-start(bf16[4,2,224,256]{3,2,1,0:T(8,128)(2,1)} %pad_maximum_fusion.1), channel_id=1, source_target_pairs={{64,0},{193,1},{128,64},{1,65},{192,128},{65,129},{0,192},{129,193... | collective-permute-start | bytes 2752520 | tf_op jit(solution)/shard_map/ppermute | solution.py:343
  33.5 38.3 %collective-permute-start.14 = (bf16[4,2,224,256]{3,2,1,0:T(8,128)(2,1)}, bf16[4,2,224,256]{3,2,1,0:T(8,128)(2,1)}, u32[]{:S(2)}, u32[]{:S(2)}) collective-permute-start(bf16[4,2,224,256]{3,2,1,0:T(8,128)(2,1)} %pad_maximum_fusion), channel_id=1, source_target_pairs={{16,0},{49,1},{32,16},{1,17},{48,32},{17,33},{0,48},{33,49},{18,2}... | collective-permute-start | bytes 2752520 | tf_op jit(solution)/shard_map/ppermute | solution.py:343
  35.7 20.8 %collective-permute-start.1 = (bf16[224,1024]{1,0:T(8,128)(2,1)S(1)}, bf16[224,1024]{1,0:T(8,128)(2,1)S(1)}, u32[]{:S(2)}, u32[]{:S(2)}) collective-permute-start(bf16[224,1024]{1,0:T(8,128)(2,1)S(1)} %get-tuple-element.23), channel_id=1, source_target_pairs={{0,4},{4,0},{1,5},{5,1},{2,6},{6,2},{3,7},{7,3},{8,12},{12,8},{9,1... | collective-permute-start | bytes 1376264 | tf_op jit(solution)/shard_map/ppermute | solution.py:337
  52.8 49.8 %collective-permute-start.13 = (bf16[4,2,224,256]{3,2,1,0:T(8,128)(2,1)}, bf16[4,2,224,256]{3,2,1,0:T(8,128)(2,1)S(1)}, u32[]{:S(2)}, u32[]{:S(2)}) collective-permute-start(bf16[4,2,224,256]{3,2,1,0:T(8,128)(2,1)} %collective-permute-done.12), channel_id=1, source_target_pairs={{0,64},{1,193},{64,128},{65,1},{128,192},{129,65},{192,0},{193,129... | collective-permute-start | bytes 2752520 | tf_op jit(solution)/shard_map/ppermute | solution.py:344
  54.7 48.0 %collective-permute-start.7 = (bf16[4,2,224,256]{3,2,1,0:T(8,128)(2,1)}, bf16[4,2,224,256]{3,2,1,0:T(8,128)(2,1)S(1)}, u32[]{:S(2)}, u32[]{:S(2)}) collective-permute-start(bf16[4,2,224,256]{3,2,1,0:T(8,128)(2,1)} %collective-permute-done.6), channel_id=1, source_target_pairs={{0,16},{1,49},{16,32},{17,1},{32,48},{33,17},{48,0},{49,33},{2,18}... | collective-permute-start | bytes 2752520 | tf_op jit(solution)/shard_map/ppermute | solution.py:344
  109.2 13.4 %collective-permute-start.16 = (bf16[4,56,512]{2,1,0:T(8,128)(2,1)S(1)}, bf16[4,56,512]{2,1,0:T(8,128)(2,1)S(1)}, u32[]{:S(2)}, u32[]{:S(2)}) collective-permute-start(bf16[4,56,512]{2,1,0:T(8,128)(2,1)S(1)} %get-tuple-element.36), channel_id=1, source_target_pairs={{0,6},{2,4},{4,2},{6,0},{1,7},{3,5},{5,3},{7,1},{8,14},{10,12},{12... | collective-permute-start | bytes 688136 | tf_op jit(solution)/shard_map/ppermute | solution.py:354
  122.4 9.2 %collective-permute-start.17 = (bf16[4,56,512]{2,1,0:T(8,128)(2,1)S(1)}, bf16[4,56,512]{2,1,0:T(8,128)(2,1)S(1)}, u32[]{:S(2)}, u32[]{:S(2)}) collective-permute-start(bf16[4,56,512]{2,1,0:T(8,128)(2,1)S(1)} %get-tuple-element.37), channel_id=1, source_target_pairs={{0,6},{2,4},{4,2},{6,0},{1,7},{3,5},{5,3},{7,1},{8,14},{10,12},{12... | collective-permute-start | bytes 688136 | tf_op jit(solution)/shard_map/ppermute | solution.py:354
